TPU v7x, 16 devices: a 4x2x1 block of a 4x4x8 slice. The times are simulated.
16 devices in a mesh: data: 2 (over y, z), tp: 8 (over x, core).
Axes of the slice: x: 4, y: 2, z: 1, core: 2. Of those that a mesh axis runs over, the one named last changes fastest.
The devices are a block of a 4x4x8 slice.
Arguments:
- X: bfloat16 [4096, 4096], P(('data', 'tp')), parts along dimension 0
- gamma: float32 [4096], replicated
- W1: bfloat16 [4096, 14336], P(None, 'tp')
- W2: bfloat16 [14336, 4096], P('tp')
- dY: bfloat16 [4096, 4096], P(('data', 'tp')), parts along dimension 0
Outputs:
- output 1: bfloat16 [4096, 4096], P(('data', 'tp')), parts along dimension 0
- output 2: bfloat16 [4096, 4096], P(('data', 'tp')), parts along dimension 0
- output 3: float32 [8192, 14336], P('data', 'tp'), parts along dimension 0
- output 4: float32 [28672, 4096], P(('data', 'tp')), parts along dimension 0
- output 5: float32 [8192], P('data'), parts along dimension 0
There are 2 independent parts. A program takes and returns all parts, laid end to end along the dimension named above; an argument that names none is the same for every part.
All inputs are finite; a program needn't handle non-finite values.
Results may differ from a plain program's by a relative error of at most 0.001.
Values are sent between devices in bfloat16 or wider.
A program may use at most 768 MiB of HBM per device.

v0:
```python
import jax
import jax.numpy as jnp
from jax import lax
from jax.sharding import PartitionSpec as P

EPS = 1e-6


def _gelu(a):
    return jax.nn.gelu(a, approximate=True)


def _ln(x):
    mu = jnp.mean(x, axis=-1, keepdims=True)
    xc = x - mu
    var = jnp.mean(xc * xc, axis=-1, keepdims=True)
    rstd = lax.rsqrt(var + EPS)
    return xc * rstd, rstd


def _tn(a, b):
    return lax.dot_general(a, b, (((0,), (0,)), ((), ())), preferred_element_type=jnp.float32)


def _nt(a, b):
    return lax.dot_general(a, b, (((1,), (1,)), ((), ())), preferred_element_type=jnp.float32)


def solution(mesh):
    rows = P(("data", "tp"), None)

    def body(X, gamma, W1, W2, dY):
        x = X.astype(jnp.float32)
        xhatv, rstd = _ln(x)
        Xn = lax.all_gather((xhatv * gamma).astype(jnp.bfloat16), "tp", axis=0, tiled=True)
        A = jnp.dot(Xn, W1, preferred_element_type=jnp.float32)
        H = _gelu(A).astype(jnp.bfloat16)
        Yp = jnp.dot(H, W2, preferred_element_type=jnp.float32)
        Y = (x + lax.psum_scatter(Yp, "tp", scatter_dimension=0, tiled=True)).astype(jnp.bfloat16)
        g = lax.all_gather(dY, "tp", axis=0, tiled=True)
        dW2 = _tn(H, g)
        dH = _nt(g, W2)
        dA = jax.vjp(_gelu, A)[1](dH)[0].astype(jnp.bfloat16)
        dW1 = _tn(Xn, dA)
        dXn = lax.psum_scatter(_nt(dA, W1), "tp", scatter_dimension=0, tiled=True)
        dgamma = lax.psum(jnp.sum(dXn * xhatv, axis=0), "tp")
        dxhat = dXn * gamma
        dx = rstd * (dxhat - jnp.mean(dxhat, axis=-1, keepdims=True) - xhatv * jnp.mean(dxhat * xhatv, axis=-1, keepdims=True))
        dX = (dY.astype(jnp.float32) + dx).astype(jnp.bfloat16)
        return Y, dX, dW1, dW2, dgamma

    return jax.shard_map(body, mesh=mesh,
                         in_specs=(rows, P(None), P(None, "tp"), P("tp", None), rows),
                         out_specs=(rows, rows, P("data", "tp"), rows, P("data")),
                         check_vma=False)
```

profile of v0, /device:TPU:112, one launch (start us, length us, event | category | flops | bytes accessed | tf_op | source)
XLA Modules:
  0.0 615.8 jit_solution(7411655733352512903)
XLA Ops:
  7.2 0.1 all-gather.5.cloned.1.call-start
  7.2 0.7 all-gather.5.cloned.1.call-update
  8.0 0.1 all-gather.3.cloned.1.call-start
  8.0 2.0 convert_reduce_fusion
  10.0 0.0 copy-start.2
  10.0 2.3 fusion.20
  12.3 0.0 copy-done.2
  12.3 0.0 copy-start.4
  12.3 0.6 copy-done.4
  12.9 3.8 fusion.13
  16.7 0.1 all-gather.3.cloned.1.call-update
  16.7 0.1 reduce-scatter.5.cloned.1.call-start
  16.8 76.8 %all-gather.5.cloned.1.call-done = bf16[2048,4096]{1,0:T(8,128)(2,1)} async-done(((bf16[256,4096]{1,0:T(8,128)(2,1)}), bf16[2048,4096]{1,0:T(8,128)(2,1)}) %all-gather.5.cloned.1.call-update) | async-done | bytes 16777232 | tf_op jit(solution)/shard_map/all_gather | solution.py:40
  93.6 39.4 %fusion.24 = f32[2048,1792]{1,0:T(8,128)} fusion(bf16[2048,4096]{1,0:T(8,128)(2,1)} %all-gather.5.cloned.1.call-done, bf16[1792,4096]{1,0:T(8,128)(2,1)} %param.8), kind=kOutput, calls=%fused_computation.35 | convolution fusion | flops 30064771072 | bytes 46137344 | tf_op jit(solution)/shard_map/dot_general | solution.py:26
  133.0 44.4 %all-gather.3.cloned.1.call-done = bf16[2048,4096]{1,0:T(8,128)(2,1)} async-done(((bf16[256,4096]{1,0:T(8,128)(2,1)}), bf16[2048,4096]{1,0:T(8,128)(2,1)}) %all-gather.3.cloned.1.call-update) | async-done | bytes 16777232 | tf_op jit(solution)/shard_map/all_gather | solution.py:35
  177.4 47.9 %fusion.6 = (bf16[2048,1792]{1,0:T(8,128)(2,1)S(1)}, f32[2048,1792]{1,0:T(8,128)}) fusion(f32[2048,1792]{1,0:T(8,128)} %fusion.24, bf16[2048,4096]{1,0:T(8,128)(2,1)} %all-gather.3.cloned.1.call-done, bf16[4096,1792]{1,0:T(8,128)(2,1)} %param.7), kind=kOutput, calls=%fused_computation.8 | convolution fusion | flops 30138171392 | bytes 68157440 | tf_op jit(solution)/shard_map/dot_general | solution.py:36
  225.3 3.0 copy-done.6
  228.4 38.2 %fusion.25 = f32[2048,4096]{1,0:T(8,128)} fusion(bf16[2048,1792]{1,0:T(8,128)(2,1)S(1)} %get-tuple-element.10, bf16[4096,1792]{1,0:T(8,128)(2,1)} %param.7), kind=kOutput, calls=%fused_computation.36 | convolution fusion | flops 30064771072 | bytes 55574528 | tf_op jit(solution)/shard_map/dot_general | solution.py:26
  266.6 0.1 reduce-scatter.5.cloned.1.call-update
  266.6 0.1 reduce-scatter.3.cloned.1.call-start
  266.7 41.7 %fusion.23 = f32[2048,4096]{1,0:T(8,128)} fusion(bf16[1792,4096]{1,0:T(8,128)(2,1)} %param.8, f32[2048,1792]{1,0:T(8,128)} %get-tuple-element.11), kind=kOutput, calls=%fused_computation.34 | convolution fusion | flops 30097801216 | bytes 62914560 | tf_op jit(solution)/shard_map/dot_general | solution.py:38
  308.3 0.1 reduce-scatter.3.cloned.1.call-update
  308.4 39.4 %fusion.26 = f32[4096,1792]{1,0:T(8,128)} fusion(bf16[2048,4096]{1,0:T(8,128)(2,1)} %all-gather.3.cloned.1.call-done, bf16[2048,1792]{1,0:T(8,128)(2,1)} %copy-done.6), kind=kOutput, calls=%fused_computation.37 | convolution fusion | flops 30064771072 | bytes 53477376 | tf_op jit(solution)/shard_map/dot_general | solution.py:22
  347.8 0.0 copy-start.5
  347.8 51.7 %fusion.22 = f32[1792,4096]{1,0:T(8,128)} fusion(bf16[2048,4096]{1,0:T(8,128)(2,1)} %all-gather.5.cloned.1.call-done, f32[2048,1792]{1,0:T(8,128)} %get-tuple-element.11), kind=kOutput, calls=%fused_computation.33 | convolution fusion | flops 30097801216 | bytes 60817408 | tf_op jit(solution)/shard_map/dot_general | solution.py:22
  399.5 34.2 %reduce-scatter.5.cloned.1.call-done = f32[256,4096]{1,0:T(8,128)} async-done(((f32[2048,4096]{1,0:T(8,128)}), f32[256,4096]{1,0:T(8,128)}) %reduce-scatter.5.cloned.1.call-update) | async-done | bytes 4194320 | tf_op jit(solution)/shard_map/reduce_scatter | solution.py:45
  433.7 0.0 copy-done
  433.7 0.0 copy-done.3
  433.7 3.9 fusion.19
  437.6 25.1 %psum.7 = f32[4096]{0:T(1024)} all-reduce(f32[4096]{0:T(1024)S(1)} %get-tuple-element.5), channel_id=1, replica_groups=mesh['data'=2,'tp'=8] {'tp'}, use_global_device_ids=true, to_apply=%region_7.0 | all-reduce | flops 4096 | bytes 32768 | tf_op jit(solution)/shard_map/psum | solution.py:46
  462.7 139.6 %reduce-scatter.3.cloned.1.call-done = f32[256,4096]{1,0:T(8,128)} async-done(((f32[2048,4096]{1,0:T(8,128)}), f32[256,4096]{1,0:T(8,128)}) %reduce-scatter.3.cloned.1.call-update) | async-done | bytes 4194320 | tf_op jit(solution)/shard_map/reduce_scatter | solution.py:39
  602.3 6.5 %fusion.18 = (bf16[256,4096]{1,0:T(8,128)(2,1)}, bf16[256,4096]{1,0:T(8,128)(2,1)}) fusion(bf16[256,4096]{1,0:T(8,128)(2,1)S(1)} %copy-done, bf16[256,4096]{1,0:T(8,128)(2,1)} %param.9, f32[256,4096]{1,0:T(8,128)} %reduce-scatter.5.cloned.1.call-done, f32[256]{0:T(256)S(1)} %get-tuple-element.12, f32[256]{0:T(256)S(1)} %get-tuple-element.13, ...), kind=kLoop, calls=%fused_computation.24 | loop fusion | flops 13631488 | bytes 16797696 | tf_op jit(solution)/shard_map/convert_element_type | solution.py:49
  (9 shorter events, 0.0 us)
Async XLA Ops:
  7.2 86.4 %all-gather.5.cloned.1.call-start = ((), (), s32[]{:S(2)}) async-start(), calls=%async_computation.4 | async-start | bytes 18874368 | tf_op jit(solution)/shard_map/all_gather | solution.py:40
  8.0 169.5 %all-gather.3.cloned.1.call-start = ((), (), s32[]{:S(2)}) async-start(), calls=%async_computation.2 | async-start | bytes 18874368 | tf_op jit(solution)/shard_map/all_gather | solution.py:35
  10.0 2.3 copy-start.2
  12.3 0.6 copy-start.4
  16.7 417.0 %reduce-scatter.5.cloned.1.call-start = ((), (), s32[]{:S(2)}) async-start(), calls=%async_computation.5 | async-start | bytes 37748736 | tf_op jit(solution)/shard_map/reduce_scatter | solution.py:45
  225.3 3.0 copy-start.6
  266.6 335.7 %reduce-scatter.3.cloned.1.call-start = ((), (), s32[]{:S(2)}) async-start(), calls=%async_computation.3 | async-start | bytes 37748736 | tf_op jit(solution)/shard_map/reduce_scatter | solution.py:39
  347.8 85.9 %copy-start = (bf16[256,4096]{1,0:T(8,128)(2,1)S(1)}, bf16[256,4096]{1,0:T(8,128)(2,1)}, u32[]{:S(2)}) copy-start(bf16[256,4096]{1,0:T(8,128)(2,1)} %param.5) | copy-start | bytes 6291460
  347.8 85.9 %copy-start.1 = (f32[4096]{0:T(1024)S(1)}, f32[4096]{0:T(1024)}, u32[]{:S(2)}) copy-start(f32[4096]{0:T(1024)} %param.6) | copy-start | bytes 49156
  347.8 85.9 %copy-start.3 = (f32[256]{0:T(256)S(1)}, f32[256]{0:T(256)}, u32[]{:S(2)}) copy-start(f32[256]{0:T(256)} %copy-done.2) | copy-start | bytes 3076
  347.8 85.9 %copy-start.5 = (f32[256]{0:T(256)S(1)}, f32[256]{0:T(256)}, u32[]{:S(2)}) copy-start(f32[256]{0:T(256)} %copy-done.4) | copy-start | bytes 3076
Sparse Core Ops, SparseCore 0:
  9.6 83.9 all-gather.4
  95.8 81.6 all-gather.2
  266.7 166.9 reduce-scatter.4
  435.9 166.3 reduce-scatter.2
where the time goes:
time: 622 us; the launch traced here: 616 us
  waiting for transfers between devices  296 us (48%)
  matrix products  258 us (41%)
  blocking collectives  25.1 us (4%)
  other arithmetic  18.4 us (3%)
  between operations  14.3 us (2%)
    reduce_scatter x1, waiting for transfers between devices, body(): lax.psum_scatter(Yp, 'tp', scatter_dimension=0, tiled=True)  140 us
    dot_general x2, matrix products, _tn(): lax.dot_general(a, b, (((0,), (0,)), ((), ())), preferred_element_type=jn...  91.1 us
    dot_general x2, matrix products, _nt(): lax.dot_general(a, b, (((1,), (1,)), ((), ())), preferred_element_type=jn...  77.6 us
    all_gather x1, waiting for transfers between devices, body(): g = lax.all_gather(dY, 'tp', axis=0, tiled=True)  76.8 us
    dot_general x1, matrix products, body(): A = jnp.dot(Xn, W1, preferred_element_type=jnp.float32)  47.9 us
    all_gather x1, waiting for transfers between devices, body(): lax.all_gather((xhatv * gamma).astype(jnp.bfloat16), 'tp', axis=0, tiled=...  44.4 us
    dot_general x1, matrix products, body(): Yp = jnp.dot(H, W2, preferred_element_type=jnp.float32)  41.7 us
    reduce_scatter x1, waiting for transfers between devices, body(): dXn = lax.psum_scatter(_nt(dA, W1), 'tp', scatter_dimension=0, tiled=True)  34.2 us
  transfers between devices with their start and end apart: 4, of which 4 were waited for; matrix products, arithmetic and copies ran while one was open for 30% of the time, Pallas kernels for 0%

commit v1 on v0

v1 whole, which is shorter than its diff:
```python
import functools

import jax
import jax.numpy as jnp
from jax import lax
from jax.experimental import pallas as pl
from jax.experimental.pallas import tpu as pltpu
from jax.sharding import PartitionSpec as P

EPS = 1e-6
BF = jnp.bfloat16
F32 = jnp.float32


def _gelu(a):
    return jax.nn.gelu(a, approximate=True)


def _ln(x):
    mu = jnp.mean(x, axis=-1, keepdims=True)
    xc = x - mu
    var = jnp.mean(xc * xc, axis=-1, keepdims=True)
    rstd = lax.rsqrt(var + EPS)
    return xc * rstd, rstd


def _tn(a, b):
    return lax.dot_general(a, b, (((0,), (0,)), ((), ())), preferred_element_type=F32)


TILE = 256
NCH = 512


def _nt(a, b):
    return lax.dot_general(a, b, (((1,), (1,)), ((), ())), preferred_element_type=F32)


def _ln_kernel(x_ref, gamma_ref, top_ref, bot_ref):
    h = top_ref.shape[0]
    gamma = gamma_ref[...]
    for out, r in ((top_ref, 0), (bot_ref, h)):
        out[...] = (_ln(x_ref[r:r + h, :].astype(F32))[0] * gamma).astype(BF)


def _norm(x, gamma):
    h = x.shape[0] // 2
    half = jax.ShapeDtypeStruct((h, x.shape[1]), BF)
    return pl.pallas_call(
        _ln_kernel, out_shape=(half, half), name="norm",
        compiler_params=pltpu.CompilerParams(vmem_limit_bytes=48 << 20),
        cost_estimate=pl.CostEstimate(flops=20 * x.size, bytes_accessed=4 * x.size, transcendentals=0),
    )(x, gamma.reshape(1, -1))


def _pass_kernel(mode, nx, nh, na, has_acc, *refs):
    refs = list(refs)

    def take(k):
        out, refs[:k] = refs[:k], []
        return out

    fwd, bwd = mode != "bwd", mode != "fwd"
    xs = take(nx) if fwd else []
    gs = take(nx) if bwd else []
    w1, w2 = take(nh), take(nh)
    a_in = [take(na) for _ in range(nh)] if not fwd else []
    y_in = take(nx) if fwd and has_acc else None
    d_in = take(nx) if bwd and has_acc else None
    a_out = take(nh) if mode == "fwd" else []
    h_out = take(nh) if fwd else []
    y_out = take(nx) if fwd else []
    da_out = take(nh) if bwd else []
    d_out = take(nx) if bwd else []
    xv = take(1)[0] if fwd else None
    gv = take(1)[0] if bwd else None

    @pl.when(pl.program_id(0) == 0)
    def _():
        for parts, v in ((xs, xv), (gs, gv)):
            r = 0
            for p in parts:
                v[r:r + p.shape[0], :] = p[...]
                r += p.shape[0]
        for outs, ins in ((y_out, y_in), (d_out, d_in)):
            for j, o in enumerate(outs):
                o[...] = ins[j][...] if ins else jnp.zeros_like(o)

    if fwd:
        a = [jnp.dot(xv[...], w1[k][...], preferred_element_type=F32) for k in range(nh)]
        h = [_gelu(v).astype(BF) for v in a]
        for k in range(nh):
            h_out[k][...] = h[k]
            if a_out:
                a_out[k][...] = a[k]
    else:
        a = [jnp.concatenate([p[...] for p in v]) for v in a_in]
    if bwd:
        dh = [_nt(gv[...], w2[k][...]) for k in range(nh)]
        da = [jax.vjp(_gelu, a[k])[1](dh[k])[0].astype(BF) for k in range(nh)]
        for k in range(nh):
            da_out[k][...] = da[k]

    def add(outs, n, v):
        r = 0
        for o in outs:
            m = o.shape[0]
            o[:, n:n + NCH] += v[r:r + m]
            r += m

    for n in range(0, w2[0].shape[1], NCH):
        if fwd:
            add(y_out, n, sum(jnp.dot(h[k], w2[k][:, n:n + NCH], preferred_element_type=F32) for k in range(nh)))
        if bwd:
            add(d_out, n, sum(_nt(da[k], w1[k][n:n + NCH, :]) for k in range(nh)))


def _pass(mode, ws, xs=(), gs=(), a=(), y=(), d=()):
    fwd, bwd = mode != "bwd", mode != "fwd"
    sizes = [p.shape[0] for p in (xs if fwd else gs)]
    nx, nh = len(sizes), len(ws)
    dm, f = ws[0][0].shape
    rows = sum(sizes)
    both = fwd + bwd
    once = pl.Buffered(buffer_count=1)

    def whole(r):
        return pl.BlockSpec((r, dm), lambda i: (0, 0), pipeline_mode=once)

    def cols(r):
        return pl.BlockSpec((r, TILE), lambda i: (0, i))

    pieces = [whole(r) for r in sizes]
    has_acc = bool(y or d)
    args = list(xs) * fwd + list(gs) * bwd + [w[0] for w in ws] + [w[1] for w in ws] + [p for v in a for p in v] + list(y) + list(d)
    in_specs = pieces * both + [cols(dm)] * nh + [pl.BlockSpec((TILE, dm), lambda i: (i, 0))] * nh
    in_specs += [cols(p.shape[0]) for v in a for p in v] + pieces * (both * has_acc)
    sums = [jax.ShapeDtypeStruct((r, dm), F32) for r in sizes]
    wide = [jax.ShapeDtypeStruct((rows, f), BF)] * nh
    outs, out_specs = (wide + sums) * both, ([cols(rows)] * nh + pieces) * both
    if mode == "fwd":
        outs, out_specs = [jax.ShapeDtypeStruct((rows, f), F32)] * nh + outs, [cols(rows)] * nh + out_specs
    outs, out_specs = outs + [jax.ShapeDtypeStruct((rows, dm), BF)] * both, out_specs + [whole(rows)] * both
    res = pl.pallas_call(
        functools.partial(_pass_kernel, mode, nx, nh, len(a[0]) if a else 0, has_acc),
        grid=(f // TILE,), in_specs=in_specs, out_specs=out_specs, out_shape=outs,
        compiler_params=pltpu.CompilerParams(vmem_limit_bytes=60 << 20, dimension_semantics=("arbitrary",)),
        cost_estimate=pl.CostEstimate(flops=4 * both * rows * dm * f * nh, transcendentals=rows * f * nh,
                                      bytes_accessed=4 * nh * dm * f + 8 * rows * dm),
    )(*args)
    out = []
    for k in [nh] * (mode == "fwd") + [nh, nx] * both + [both]:
        out.append(list(res[:k]))
        res = res[k:]
    return out


def solution(mesh):
    rows = P(("data", "tp"), None)
    n = mesh.shape["tp"]
    up = [(i, (i + 2) % n) for i in range(n)]
    down = [(i, (i - 2) % n) for i in range(n)]
    over = [(i, (i + 4) % n) for i in range(n)]
    swap = [(i, i ^ 1) for i in range(n)]
    cat = jnp.concatenate

    def body(X, gamma, W1, W2, dY):
        last = [None]

        def step(f, *args):
            if last[0] is not None:
                args, _ = lax.optimization_barrier((args, last[0]))
            out = f(*args)
            last[0] = jax.tree.leaves(out)[0]
            return out

        def send(v, perm):
            if last[0] is not None:
                v, _ = lax.optimization_barrier((v, last[0]))
            return lax.ppermute(v, "tp", perm)

        h = X.shape[0] // 2
        W1p = send(W1, swap)
        g = step(lambda v: (v[:h], v[h:]), dY)
        g0u = send(g[0], up)
        g0d = send(g[1], down)
        xn = step(_norm, X, gamma)
        x0u = send(xn[0], up)
        x0d = send(xn[1], down)
        x1u = send(xn[1], up)
        x1d = send(xn[0], down)
        W2p = send(W2, swap)

        Hoa, Yo, dAoa, dXo, (Xo, _) = step(lambda x, g, w: _pass("both", [w], xs=x, gs=g), xn, g, (W1, W2))
        x2u = send(x0u, up)
        x2d = send(x0d, down)
        g1u = send(g[1], up)
        g1d = send(g[0], down)
        g2u = send(g0u, up)
        g2d = send(g0d, down)
        Gp0 = send(dY, swap)
        Xp0 = send(Xo, swap)

        ws = [(W1, W2), (W1p, W2p)]
        Ae, He, Ye, (Xe,) = step(lambda x, w: _pass("fwd", w, xs=x), (x1d, x0d, x0u, x1u), ws)
        Xp1 = send(Xe, swap)
        Hp1 = send(He[1], swap)
        Af, Hf, Yf, (Xf,) = step(lambda x, w: _pass("fwd", w, xs=x), (x2u, x2d), ws)
        yfu = send(Yf[0], up)
        yfd = send(Yf[1], down)
        ypu = send(Ye[1], up)
        ypd = send(Ye[2], down)
        Xp2 = send(Xf, swap)
        Hp2 = send(Hf[1], swap)

        dAr, dXr, (Gr,) = step(lambda g, w, a: _pass("bwd", w, gs=g, a=a),
                               (g1d, g0d, g0u, g1u, g2u, g2d), ws, list(zip(Ae, Af)))
        xfu = send(dXr[4], up)
        xfd = send(dXr[5], down)
        xpu = send(dXr[1], up)
        xpd = send(dXr[2], down)
        Dp1 = send(dAr[1], swap)
        Gp1 = send(Gr, swap)

        Hob, Yo, dAob, dXo, _ = step(lambda x, g, w, y, d: _pass("both", [w], xs=x, gs=g, y=y, d=d),
                                     xn, g, (W1p, W2p), Yo, dXo)
        Hp0 = send(Hob[0], swap)
        Dp0 = send(dAob[0], swap)

        dW1 = step(lambda a, b: _tn(cat(a), cat(b)), [Xo, Xe, Xf, Xp0, Xp1, Xp2], [dAoa[0], dAr[0], Dp0, Dp1])

        add2 = lambda a, b, u, d: (a + u, b + d)
        xqu, xqd = step(add2, dXr[0], dXr[3], xfu, xfd)
        xqu = send(xqu, up)
        xqd = send(xqd, down)
        yqu, yqd = step(add2, Ye[0], Ye[3], yfu, yfd)
        yqu = send(yqu, up)
        yqd = send(yqd, down)
        dW2 = step(lambda a, b: _tn(cat(a), cat(b)), [Hoa[0], He[0], Hf[0], Hp0, Hp1, Hp2], [dY, Gr, Gp0, Gp1])

        Yt = step(lambda yo, u, d: X.astype(F32) + (cat(yo) + cat([d, u])), Yo, ypu, ypd)

        def fin(dxo, xpu, xqu, xpd, xqd):
            dXn = cat(dxo) + cat([xqu, xpu]) + cat([xpd, xqd])
            xhatv, rstd = _ln(X.astype(F32))
            dgam = jnp.sum(dXn * xhatv, axis=0, keepdims=True)
            dxhat = dXn * gamma
            dx = rstd * (dxhat - jnp.mean(dxhat, axis=-1, keepdims=True) - xhatv * jnp.mean(dxhat * xhatv, axis=-1, keepdims=True))
            return (dY.astype(F32) + dx).astype(BF), dgam

        dX, dgam = step(fin, dXo, xpu, xqu, xpd, xqd)
        dgam = step(lambda a, b: a + b, dgam, send(dgam, swap))
        dgs = send(dgam, up), send(dgam, down), send(dgam, over)

        Y = step(lambda t, u, d: (t + cat([u, d])).astype(BF), Yt, yqu, yqd)
        dgam = dgam + dgs[0] + dgs[1] + dgs[2]
        return Y, dX, dW1, dW2, dgam[0]

    return jax.shard_map(body, mesh=mesh,
                         in_specs=(rows, P(None), P(None, "tp"), P("tp", None), rows),
                         out_specs=(rows, rows, P("data", "tp"), rows, P("data")),
                         check_vma=False)
```

time: 622 us -> 606 us (0.974)
  Pallas kernels: 0 us -> 201 us
  matrix products: 258 us -> 78 us
  waiting for transfers between devices: 296 us -> 246 us
  starting transfers between devices: 0.25 us -> 32.3 us
  blocking collectives: 25.1 us -> 0 us
  local copies, waits for them, and re-layouts: 3.63 us -> 20.4 us
  between operations: 14.3 us -> 1.6 us
    ppermute x0 -> x40, waiting for transfers between devices: none -> 246 us  [send(): return lax.ppermute(v, 'tp', perm)]
    pallas_call x0 -> x6, Pallas kernels: none -> 201 us  [the longest x5 198 us: _pass(): pl.pallas_call(functools.partial(_pass_kernel, mode, nx, nh, len(a[0]) if...]
    dot_general x6 -> x2, matrix products: 258 us -> 78 us  [_tn(): lax.dot_general(a, b, (((0,), (0,)), ((), ())), preferred_element_type=F32)]
    reduce_scatter x2 -> x0, waiting for transfers between devices: 174 us -> none  [the longest x1 140 us: body(): lax.psum_scatter(Yp, 'tp', scatter_dimension=0, tiled=True)]
    all_gather x2 -> x0, waiting for transfers between devices: 121 us -> none  [the longest x1 76.8 us: body(): g = lax.all_gather(dY, 'tp', axis=0, tiled=True)]
    ppermute x0 -> x40, starting transfers between devices: none -> 32.3 us  [send(): return lax.ppermute(v, 'tp', perm)]
    psum x1 -> x0, blocking collectives: 25.1 us -> none  [body(): dgamma = lax.psum(jnp.sum(dXn * xhatv, axis=0), 'tp')]
    unnamed x14 -> x58, local copies, waits for them, and re-layouts: 3.63 us -> 15.7 us
  transfers between devices with their start and end apart: 4 -> 40, of which waited for: 4 -> 13; matrix products, arithmetic and copies ran while one was open for 30% -> 19% of each run, Pallas kernels for 0% -> 33%
where the time goes in v1:
time: 606 us; the launch traced here: 603 us
  waiting for transfers between devices  246 us (41%)
  Pallas kernels  201 us (33%)
  matrix products  78 us (13%)
  starting transfers between devices  32.3 us (5%)
  other arithmetic  23.9 us (4%)
  local copies, waits for them, and re-layouts  20.4 us (3%)
    ppermute x40, waiting for transfers between devices, send(): return lax.ppermute(v, 'tp', perm)  246 us
    pallas_call x5, Pallas kernels, _pass(): pl.pallas_call(functools.partial(_pass_kernel, mode, nx, nh, len(a[0]) if...  198 us
    dot_general x2, matrix products, _tn(): lax.dot_general(a, b, (((0,), (0,)), ((), ())), preferred_element_type=F32)  78 us
    ppermute x40, starting transfers between devices, send(): return lax.ppermute(v, 'tp', perm)  32.3 us
    unnamed x58, local copies, waits for them, and re-layouts  15.7 us
  transfers between devices with their start and end apart: 40, of which 13 were waited for; matrix products, arithmetic and copies ran while one was open for 19% of the time, Pallas kernels for 33%

profile of v1, /device:TPU:112, one launch (start us, length us, event | category | flops | bytes accessed | tf_op | source)
XLA Modules:
  0.0 603.2 jit_solution(14204024730510278770)
XLA Ops:
  0.7 2.9 fusion.33
  3.5 2.7 norm.1
  6.7 3.9 collective-permute-start.9
  11.1 22.4 %collective-permute-done.9.refs_1_ = bf16[128,4096]{1,0:T(8,128)(2,1)S(1)} collective-permute-done((bf16[128,4096]{1,0:T(8,128)(2,1)}, bf16[128,4096]{1,0:T(8,128)(2,1)S(1)}, u32[]{:S(2)}, u32[]{:S(2)}) %collective-permute-start.9) | collective-permute-done | bytes 1048608 | tf_op jit(solution)/shard_map/ppermute | solution.py:180
  34.3 3.5 collective-permute-done.10.refs_2_
  37.9 22.5 %collective-permute-done.4.refs_2_ = bf16[128,4096]{1,0:T(8,128)(2,1)S(1)} collective-permute-done((bf16[128,4096]{1,0:T(8,128)(2,1)S(1)}, bf16[128,4096]{1,0:T(8,128)(2,1)S(1)}, u32[]{:S(2)}, u32[]{:S(2)}) %collective-permute-start.4) | collective-permute-done | bytes 1048608 | tf_op jit(solution)/shard_map/ppermute | solution.py:180
  61.3 26.9 %shard_map.92 = (bf16[256,1792]{1,0:T(8,128)(2,1)}, f32[128,4096]{1,0:T(8,128)}, f32[128,4096]{1,0:T(8,128)}, bf16[256,1792]{1,0:T(8,128)(2,1)}, f32[128,4096]{1...) custom-call(bf16[128,4096]{1,0:T(8,128)(2,1)} %copy-done.3, ...), custom_call_target="tpu_custom_call" | custom-call | flops 15032385536 | bytes 37748736 | tf_op jit(solution)/shard_map/pallas_call | solution.py:144
  88.4 2.1 collective-permute-start.5
  92.5 1.9 collective-permute-start.6
  94.4 44.9 %shard_map.93 = (f32[512,1792]{1,0:T(8,128)}, f32[512,1792]{1,0:T(8,128)}, bf16[512,1792]{1,0:T(8,128)(2,1)}, bf16[512,1792]{1,0:T(8,128)(2,1)}, f32[128,4096]{1...) custom-call(bf16[128,4096]{1,0:T(8,128)(2,1)} %collective-permute-done, ...), custom_call_target="tpu_custom_call" | custom-call | flops 30064771072 | bytes 75497472 | tf_op jit(solution)/shard_map/pallas_call | solution.py:144
  140.7 29.2 %shard_map.94 = (f32[256,1792]{1,0:T(8,128)}, f32[256,1792]{1,0:T(8,128)}, bf16[256,1792]{1,0:T(8,128)(2,1)}, bf16[256,1792]{1,0:T(8,128)(2,1)}, f32[128,4096]{1...) custom-call(bf16[128,4096]{1,0:T(8,128)(2,1)} %collective-permute-done.12.refs_0_, ...), custom_call_target="tpu_custom_call" | custom-call | flops 15032385536 | bytes 67108864 | tf_op jit(solution)/shard_map/pallas_call | solution.py:144
  170.1 67.6 %shard_map.95 = (bf16[768,1792]{1,0:T(8,128)(2,1)}, bf16[768,1792]{1,0:T(8,128)(2,1)}, f32[128,4096]{1,0:T(8,128)}, f32[128,4096]{1,0:T(8,128)}, f32[128,4096]{1...) custom-call(bf16[128,4096]{1,0:T(8,128)(2,1)} %collective-permute-done, ...), custom_call_target="tpu_custom_call" | custom-call | flops 45097156608 | bytes 83886080 | tf_op jit(solution)/shard_map/pallas_call | solution.py:144
  238.8 29.8 %shard_map.96 = (bf16[256,1792]{1,0:T(8,128)(2,1)}, f32[128,4096]{1,0:T(8,128)}, f32[128,4096]{1,0:T(8,128)}, bf16[256,1792]{1,0:T(8,128)(2,1)}, f32[128,4096]{1...) custom-call(bf16[128,4096]{1,0:T(8,128)(2,1)} %copy-done.3, ...), custom_call_target="tpu_custom_call" | custom-call | flops 15032385536 | bytes 37748736 | tf_op jit(solution)/shard_map/pallas_call | solution.py:144
  273.4 2.5 collective-permute-start.22
  281.1 2.5 constant_dynamic-update-slice_fusion.1
  285.4 34.6 %collective-permute-done.24 = f32[128,4096]{1,0:T(8,128)S(1)} collective-permute-done((f32[128,4096]{1,0:T(8,128)}, f32[128,4096]{1,0:T(8,128)S(1)}, u32[]{:S(2)}, u32[]{:S(2)}) %collective-permute-start.24) | collective-permute-done | bytes 2097184 | tf_op jit(solution)/shard_map/ppermute | solution.py:180
  320.0 2.6 collective-permute-done.23
  322.6 41.7 %collective-permute-done.22 = f32[128,4096]{1,0:T(8,128)} collective-permute-done((f32[128,4096]{1,0:T(8,128)}, f32[128,4096]{1,0:T(8,128)}, u32[]{:S(2)}, u32[]{:S(2)}) %collective-permute-start.22) | collective-permute-done | bytes 2097184 | tf_op jit(solution)/shard_map/ppermute | solution.py:180
  364.3 2.2 collective-permute-done.21
  366.7 39.3 %fusion.8 = f32[4096,1792]{1,0:T(8,128)} fusion(bf16[2048,4096]{1,0:T(8,128)(2,1)} %copy-done.18, bf16[768,1792]{1,0:T(8,128)(2,1)} %collective-permute-done.29, bf16[256,1792]{1,0:T(8,128)(2,1)} %copy-done.23, bf16[768,1792]{1,0:T(8,128)(2,1)} %get-tuple-element.285, bf16[256,1792]{1,0:T(8,128)(2,1)} %get-tuple-element.284), kind=kOutput, calls=%fused_computation.8 | convolution fusion | flops 30094131200 | bytes 53477376 | tf_op jit(solution)/shard_map/dot_general | solution.py:28
  406.0 3.3 add.53
  413.6 2.0 add.57
  417.6 3.1 collective-permute-start.34
  424.4 2.9 copy-done.19
  429.0 38.7 %fusion = f32[1792,4096]{1,0:T(8,128)} fusion(bf16[2048,1792]{1,0:T(8,128)(2,1)} %copy-done.19, bf16[768,4096]{1,0:T(8,128)(2,1)} %collective-permute-done.20, bf16[256,4096]{1,0:T(8,128)(2,1)} %collective-permute-done.19, bf16[768,4096]{1,0:T(8,128)(2,1)} %get-tuple-element.299, bf16[256,4096]{1,0:T(8,128)(2,1)S(1)} %copy-done.4), kind=kOutput, calls=%fused_computation | convolution fusion | flops 30131879936 | bytes 53477376 | tf_op jit(solution)/shard_map/dot_general | solution.py:28
  469.2 4.1 fusion.27
  473.3 37.4 %collective-permute-done.32 = f32[128,4096]{1,0:T(8,128)} collective-permute-done((f32[128,4096]{1,0:T(8,128)}, f32[128,4096]{1,0:T(8,128)}, u32[]{:S(2)}, u32[]{:S(2)}) %collective-permute-start.32) | collective-permute-done | bytes 2097184 | tf_op jit(solution)/shard_map/ppermute | solution.py:180
  512.0 43.6 %collective-permute-done.33 = f32[128,4096]{1,0:T(8,128)} collective-permute-done((f32[128,4096]{1,0:T(8,128)}, f32[128,4096]{1,0:T(8,128)}, u32[]{:S(2)}, u32[]{:S(2)}) %collective-permute-start.33) | collective-permute-done | bytes 2097184 | tf_op jit(solution)/shard_map/ppermute | solution.py:180
  555.6 4.7 fusion.22
  560.4 3.4 fusion.26
  565.7 2.7 collective-permute-start.38
  568.4 31.9 %collective-permute-done.30 = f32[128,4096]{1,0:T(8,128)S(1)} collective-permute-done((f32[128,4096]{1,0:T(8,128)S(1)}, f32[128,4096]{1,0:T(8,128)S(1)}, u32[]{:S(2)}, u32[]{:S(2)}) %collective-permute-start.30) | collective-permute-done | bytes 2097184 | tf_op jit(solution)/shard_map/ppermute | solution.py:180
  (131 shorter events, 38.3 us)
Async XLA Ops:
  6.2 85.5 %collective-permute-start.1 = (bf16[1792,4096]{1,0:T(8,128)(2,1)}, bf16[1792,4096]{1,0:T(8,128)(2,1)}, u32[]{:S(2)}, u32[]{:S(2)}) collective-permute-start(bf16[1792,4096]{1,0:T(8,128)(2,1)} %refs_8_), channel_id=1, source_target_pairs={{0,1},{1,0},{2,3},{3,2},{4,5},{5,4},{6,7},{7,6},{8,9},{9,8},{10,11... | collective-permute-start | bytes 44040200 | tf_op jit(solution)/shard_map/ppermute | solution.py:180
  6.2 86.3 %collective-permute-start = (bf16[4096,1792]{1,0:T(8,128)(2,1)}, bf16[4096,1792]{1,0:T(8,128)(2,1)}, u32[]{:S(2)}, u32[]{:S(2)}) collective-permute-start(bf16[4096,1792]{1,0:T(8,128)(2,1)} %refs_6_.1), channel_id=1, source_target_pairs={{0,1},{1,0},{2,3},{3,2},{4,5},{5,4},{6,7},{7,6},{8,9},{9,8},{10,11... | collective-permute-start | bytes 44040200 | tf_op jit(solution)/shard_map/ppermute | solution.py:180
  10.6 49.7 %collective-permute-start.4 = (bf16[128,4096]{1,0:T(8,128)(2,1)S(1)}, bf16[128,4096]{1,0:T(8,128)(2,1)S(1)}, u32[]{:S(2)}, u32[]{:S(2)}) collective-permute-start(bf16[128,4096]{1,0:T(8,128)(2,1)S(1)} %get-tuple-element.230.refs_2_), channel_id=1, source_target_pairs={{0,2},{1,3},{2,4},{3,5},{4,6},{5,7},{6,0},{7,1},{8,10},{9,11},{10,... | collective-permute-start | bytes 3145736 | tf_op jit(solution)/shard_map/ppermute | solution.py:180
  33.5 54.9 %collective-permute-start.11 = (bf16[128,4096]{1,0:T(8,128)(2,1)}, bf16[128,4096]{1,0:T(8,128)(2,1)}, u32[]{:S(2)}, u32[]{:S(2)}) collective-permute-start(bf16[128,4096]{1,0:T(8,128)(2,1)} %get-tuple-element.229.refs_1_), channel_id=1, source_target_pairs={{0,2},{1,3},{2,4},{3,5},{4,6},{5,7},{6,0},{7,1},{8,10},{9,11},{10,... | collective-permute-start | bytes 3145736 | tf_op jit(solution)/shard_map/ppermute | solution.py:180
  37.9 52.6 %collective-permute-start.8 = (bf16[128,4096]{1,0:T(8,128)(2,1)S(1)}, bf16[128,4096]{1,0:T(8,128)(2,1)}, u32[]{:S(2)}, u32[]{:S(2)}) collective-permute-start(bf16[128,4096]{1,0:T(8,128)(2,1)S(1)} %get-tuple-element.228.refs_0_), channel_id=1, source_target_pairs={{0,6},{1,7},{2,0},{3,1},{4,2},{5,3},{6,4},{7,5},{8,14},{9,15},{10,... | collective-permute-start | bytes 3145736 | tf_op jit(solution)/shard_map/ppermute | solution.py:180
  88.3 81.7 %collective-permute-start.2 = (bf16[128,4096]{1,0:T(8,128)(2,1)}, bf16[128,4096]{1,0:T(8,128)(2,1)}, u32[]{:S(2)}, u32[]{:S(2)}) collective-permute-start(bf16[128,4096]{1,0:T(8,128)(2,1)} %copy-done.14), channel_id=1, source_target_pairs={{0,6},{1,7},{2,0},{3,1},{4,2},{5,3},{6,4},{7,5},{8,14},{9,15},{10,... | collective-permute-start | bytes 3145736 | tf_op jit(solution)/shard_map/ppermute | solution.py:180
  88.4 81.6 %collective-permute-start.5 = (bf16[128,4096]{1,0:T(8,128)(2,1)}, bf16[128,4096]{1,0:T(8,128)(2,1)}, u32[]{:S(2)}, u32[]{:S(2)}) collective-permute-start(bf16[128,4096]{1,0:T(8,128)(2,1)} %get-tuple-element.231.refs_3_), channel_id=1, source_target_pairs={{0,2},{1,3},{2,4},{3,5},{4,6},{5,7},{6,0},{7,1},{8,10},{9,11},{10,... | collective-permute-start | bytes 3145736 | tf_op jit(solution)/shard_map/ppermute | solution.py:180
  90.5 48.8 %collective-permute-start.13 = (bf16[128,4096]{1,0:T(8,128)(2,1)}, bf16[128,4096]{1,0:T(8,128)(2,1)S(1)}, u32[]{:S(2)}, u32[]{:S(2)}) collective-permute-start(bf16[128,4096]{1,0:T(8,128)(2,1)} %copy-done.22), channel_id=1, source_target_pairs={{0,6},{1,7},{2,0},{3,1},{4,2},{5,3},{6,4},{7,5},{8,14},{9,15},{10,... | collective-permute-start | bytes 3145736 | tf_op jit(solution)/shard_map/ppermute | solution.py:180
  91.7 49.0 %collective-permute-start.12 = (bf16[128,4096]{1,0:T(8,128)(2,1)}, bf16[128,4096]{1,0:T(8,128)(2,1)}, u32[]{:S(2)}, u32[]{:S(2)}) collective-permute-start(bf16[128,4096]{1,0:T(8,128)(2,1)} %copy-done.21), channel_id=1, source_target_pairs={{0,2},{1,3},{2,4},{3,5},{4,6},{5,7},{6,0},{7,1},{8,10},{9,11},{10,... | collective-permute-start | bytes 3145736 | tf_op jit(solution)/shard_map/ppermute | solution.py:180
  92.5 77.5 %collective-permute-start.6 = (bf16[128,4096]{1,0:T(8,128)(2,1)}, bf16[128,4096]{1,0:T(8,128)(2,1)}, u32[]{:S(2)}, u32[]{:S(2)}) collective-permute-start(bf16[128,4096]{1,0:T(8,128)(2,1)} %copy-done.20), channel_id=1, source_target_pairs={{0,2},{1,3},{2,4},{3,5},{4,6},{5,7},{6,0},{7,1},{8,10},{9,11},{10,... | collective-permute-start | bytes 3145736 | tf_op jit(solution)/shard_map/ppermute | solution.py:180
  170.0 105.8 %collective-permute-start.26 = (bf16[512,4096]{1,0:T(8,128)(2,1)}, bf16[512,4096]{1,0:T(8,128)(2,1)}, u32[]{:S(2)}, u32[]{:S(2)}) collective-permute-start(bf16[512,4096]{1,0:T(8,128)(2,1)} %get-tuple-element.279), channel_id=1, source_target_pairs={{0,1},{1,0},{2,3},{3,2},{4,5},{5,4},{6,7},{7,6},{8,9},{9,8},{10,11... | collective-permute-start | bytes 12582920 | tf_op jit(solution)/shard_map/ppermute | solution.py:180
  237.7 35.6 %collective-permute-start.29 = (bf16[768,1792]{1,0:T(8,128)(2,1)}, bf16[768,1792]{1,0:T(8,128)(2,1)}, u32[]{:S(2)}, u32[]{:S(2)}) collective-permute-start(bf16[768,1792]{1,0:T(8,128)(2,1)} %get-tuple-element.277), channel_id=1, source_target_pairs={{0,1},{1,0},{2,3},{3,2},{4,5},{5,4},{6,7},{7,6},{8,9},{9,8},{10,11... | collective-permute-start | bytes 8257544 | tf_op jit(solution)/shard_map/ppermute | solution.py:180
  238.4 34.2 %collective-permute-start.27 = (bf16[256,4096]{1,0:T(8,128)(2,1)}, bf16[256,4096]{1,0:T(8,128)(2,1)}, u32[]{:S(2)}, u32[]{:S(2)}) collective-permute-start(bf16[256,4096]{1,0:T(8,128)(2,1)} %get-tuple-element.280), channel_id=1, source_target_pairs={{0,1},{1,0},{2,3},{3,2},{4,5},{5,4},{6,7},{7,6},{8,9},{9,8},{10,11... | collective-permute-start | bytes 6291464 | tf_op jit(solution)/shard_map/ppermute | solution.py:180
  271.3 48.7 %collective-permute-start.24 = (f32[128,4096]{1,0:T(8,128)}, f32[128,4096]{1,0:T(8,128)S(1)}, u32[]{:S(2)}, u32[]{:S(2)}) collective-permute-start(f32[128,4096]{1,0:T(8,128)} %get-tuple-element.266), channel_id=1, source_target_pairs={{0,6},{1,7},{2,0},{3,1},{4,2},{5,3},{6,4},{7,5},{8,14},{9,15},{10,... | collective-permute-start | bytes 6291464 | tf_op jit(solution)/shard_map/ppermute | solution.py:180
  272.6 50.0 %collective-permute-start.23 = (f32[128,4096]{1,0:T(8,128)}, f32[128,4096]{1,0:T(8,128)}, u32[]{:S(2)}, u32[]{:S(2)}) collective-permute-start(f32[128,4096]{1,0:T(8,128)} %get-tuple-element.264), channel_id=1, source_target_pairs={{0,2},{1,3},{2,4},{3,5},{4,6},{5,7},{6,0},{7,1},{8,10},{9,11},{10,... | collective-permute-start | bytes 6291464 | tf_op jit(solution)/shard_map/ppermute | solution.py:180
  273.4 90.9 %collective-permute-start.22 = (f32[128,4096]{1,0:T(8,128)}, f32[128,4096]{1,0:T(8,128)}, u32[]{:S(2)}, u32[]{:S(2)}) collective-permute-start(f32[128,4096]{1,0:T(8,128)} %get-tuple-element.260), channel_id=1, source_target_pairs={{0,6},{1,7},{2,0},{3,1},{4,2},{5,3},{6,4},{7,5},{8,14},{9,15},{10,... | collective-permute-start | bytes 6291464 | tf_op jit(solution)/shard_map/ppermute | solution.py:180
  275.8 90.6 %collective-permute-start.21 = (f32[128,4096]{1,0:T(8,128)}, f32[128,4096]{1,0:T(8,128)}, u32[]{:S(2)}, u32[]{:S(2)}) collective-permute-start(f32[128,4096]{1,0:T(8,128)} %get-tuple-element.258), channel_id=1, source_target_pairs={{0,2},{1,3},{2,4},{3,5},{4,6},{5,7},{6,0},{7,1},{8,10},{9,11},{10,... | collective-permute-start | bytes 6291464 | tf_op jit(solution)/shard_map/ppermute | solution.py:180
  285.3 135.4 %collective-permute-start.20 = (bf16[768,4096]{1,0:T(8,128)(2,1)}, bf16[768,4096]{1,0:T(8,128)(2,1)}, u32[]{:S(2)}, u32[]{:S(2)}) collective-permute-start(bf16[768,4096]{1,0:T(8,128)(2,1)} %get-tuple-element.299), channel_id=1, source_target_pairs={{0,1},{1,0},{2,3},{3,2},{4,5},{5,4},{6,7},{7,6},{8,9},{9,8},{10,11... | collective-permute-start | bytes 18874376 | tf_op jit(solution)/shard_map/ppermute | solution.py:180
  320.0 95.6 %collective-permute-start.18 = (bf16[256,1792]{1,0:T(8,128)(2,1)}, bf16[256,1792]{1,0:T(8,128)(2,1)S(1)}, u32[]{:S(2)}, u32[]{:S(2)}) collective-permute-start(bf16[256,1792]{1,0:T(8,128)(2,1)} %get-tuple-element.251), channel_id=1, source_target_pairs={{0,1},{1,0},{2,3},{3,2},{4,5},{5,4},{6,7},{7,6},{8,9},{9,8},{10,11... | collective-permute-start | bytes 2752520 | tf_op jit(solution)/shard_map/ppermute | solution.py:180
  322.6 95.0 %collective-permute-start.17 = (bf16[512,1792]{1,0:T(8,128)(2,1)}, bf16[512,1792]{1,0:T(8,128)(2,1)}, u32[]{:S(2)}, u32[]{:S(2)}) collective-permute-start(bf16[512,1792]{1,0:T(8,128)(2,1)} %get-tuple-element.249), channel_id=1, source_target_pairs={{0,1},{1,0},{2,3},{3,2},{4,5},{5,4},{6,7},{7,6},{8,9},{9,8},{10,11... | collective-permute-start | bytes 5505032 | tf_op jit(solution)/shard_map/ppermute | solution.py:180
  364.3 53.2 %collective-permute-start.16 = (bf16[256,1792]{1,0:T(8,128)(2,1)}, bf16[256,1792]{1,0:T(8,128)(2,1)}, u32[]{:S(2)}, u32[]{:S(2)}) collective-permute-start(bf16[256,1792]{1,0:T(8,128)(2,1)} %get-tuple-element.247), channel_id=1, source_target_pairs={{0,1},{1,0},{2,3},{3,2},{4,5},{5,4},{6,7},{7,6},{8,9},{9,8},{10,11... | collective-permute-start | bytes 2752520 | tf_op jit(solution)/shard_map/ppermute | solution.py:180
  366.4 60.8 %collective-permute-start.15 = (f32[128,4096]{1,0:T(8,128)}, f32[128,4096]{1,0:T(8,128)}, u32[]{:S(2)}, u32[]{:S(2)}) collective-permute-start(f32[128,4096]{1,0:T(8,128)} %get-tuple-element.243), channel_id=1, source_target_pairs={{0,6},{1,7},{2,0},{3,1},{4,2},{5,3},{6,4},{7,5},{8,14},{9,15},{10,... | collective-permute-start | bytes 6291464 | tf_op jit(solution)/shard_map/ppermute | solution.py:180
  415.6 52.1 %collective-permute-start.14 = (f32[128,4096]{1,0:T(8,128)}, f32[128,4096]{1,0:T(8,128)}, u32[]{:S(2)}, u32[]{:S(2)}) collective-permute-start(f32[128,4096]{1,0:T(8,128)} %get-tuple-element.241), channel_id=1, source_target_pairs={{0,2},{1,3},{2,4},{3,5},{4,6},{5,7},{6,0},{7,1},{8,10},{9,11},{10,... | collective-permute-start | bytes 6291464 | tf_op jit(solution)/shard_map/ppermute | solution.py:180
  417.5 93.2 %collective-permute-start.32 = (f32[128,4096]{1,0:T(8,128)}, f32[128,4096]{1,0:T(8,128)}, u32[]{:S(2)}, u32[]{:S(2)}) collective-permute-start(f32[128,4096]{1,0:T(8,128)} %get-tuple-element.313), channel_id=1, source_target_pairs={{0,2},{1,3},{2,4},{3,5},{4,6},{5,7},{6,0},{7,1},{8,10},{9,11},{10,... | collective-permute-start | bytes 6291464 | tf_op jit(solution)/shard_map/ppermute | solution.py:180
  417.6 93.6 %collective-permute-start.34 = (f32[128,4096]{1,0:T(8,128)}, f32[128,4096]{1,0:T(8,128)}, u32[]{:S(2)}, u32[]{:S(2)}) collective-permute-start(f32[128,4096]{1,0:T(8,128)} %get-tuple-element.316), channel_id=1, source_target_pairs={{0,6},{1,7},{2,0},{3,1},{4,2},{5,3},{6,4},{7,5},{8,14},{9,15},{10,... | collective-permute-start | bytes 6291464 | tf_op jit(solution)/shard_map/ppermute | solution.py:180
  420.7 91.3 %collective-permute-start.35 = (f32[128,4096]{1,0:T(8,128)}, f32[128,4096]{1,0:T(8,128)}, u32[]{:S(2)}, u32[]{:S(2)}) collective-permute-start(f32[128,4096]{1,0:T(8,128)} %add.58), channel_id=1, source_target_pairs={{0,6},{1,7},{2,0},{3,1},{4,2},{5,3},{6,4},{7,5},{8,14},{9,15},{10,... | collective-permute-start | bytes 6291464 | tf_op jit(solution)/shard_map/ppermute | solution.py:180
  427.3 128.4 %collective-permute-start.33 = (f32[128,4096]{1,0:T(8,128)}, f32[128,4096]{1,0:T(8,128)}, u32[]{:S(2)}, u32[]{:S(2)}) collective-permute-start(f32[128,4096]{1,0:T(8,128)} %add.53), channel_id=1, source_target_pairs={{0,2},{1,3},{2,4},{3,5},{4,6},{5,7},{6,0},{7,1},{8,10},{9,11},{10,... | collective-permute-start | bytes 6291464 | tf_op jit(solution)/shard_map/ppermute | solution.py:180
  467.7 100.6 %collective-permute-start.31 = (f32[128,4096]{1,0:T(8,128)S(1)}, f32[128,4096]{1,0:T(8,128)S(1)}, u32[]{:S(2)}, u32[]{:S(2)}) collective-permute-start(f32[128,4096]{1,0:T(8,128)S(1)} %add.57), channel_id=1, source_target_pairs={{0,6},{1,7},{2,0},{3,1},{4,2},{5,3},{6,4},{7,5},{8,14},{9,15},{10,... | collective-permute-start | bytes 6291464 | tf_op jit(solution)/shard_map/ppermute | solution.py:180
  510.7 89.6 %collective-permute-start.30 = (f32[128,4096]{1,0:T(8,128)S(1)}, f32[128,4096]{1,0:T(8,128)S(1)}, u32[]{:S(2)}, u32[]{:S(2)}) collective-permute-start(f32[128,4096]{1,0:T(8,128)S(1)} %add.54), channel_id=1, source_target_pairs={{0,2},{1,3},{2,4},{3,5},{4,6},{5,7},{6,0},{7,1},{8,10},{9,11},{10,... | collective-permute-start | bytes 6291464 | tf_op jit(solution)/shard_map/ppermute | solution.py:180
  565.0 37.0 %collective-permute-start.37 = (f32[1,4096]{1,0:T(1,128)S(1)}, f32[1,4096]{1,0:T(1,128)S(1)}, u32[]{:S(2)}, u32[]{:S(2)}) collective-permute-start(f32[1,4096]{1,0:T(1,128)S(1)} %add.64), channel_id=1, source_target_pairs={{0,2},{1,3},{2,4},{3,5},{4,6},{5,7},{6,0},{7,1},{8,10},{9,11},{10,... | collective-permute-start | bytes 49160 | tf_op jit(solution)/shard_map/ppermute | solution.py:180
  565.7 36.4 %collective-permute-start.38 = (f32[1,4096]{1,0:T(1,128)S(1)}, f32[1,4096]{1,0:T(1,128)S(1)}, u32[]{:S(2)}, u32[]{:S(2)}) collective-permute-start(f32[1,4096]{1,0:T(1,128)S(1)} %add.64), channel_id=1, source_target_pairs={{0,6},{1,7},{2,0},{3,1},{4,2},{5,3},{6,4},{7,5},{8,14},{9,15},{10,... | collective-permute-start | bytes 49160 | tf_op jit(solution)/shard_map/ppermute | solution.py:180
  568.3 33.7 %collective-permute-start.39 = (f32[1,4096]{1,0:T(1,128)S(1)}, f32[1,4096]{1,0:T(1,128)S(1)}, u32[]{:S(2)}, u32[]{:S(2)}) collective-permute-start(f32[1,4096]{1,0:T(1,128)S(1)} %add.64), channel_id=1, source_target_pairs={{0,4},{1,5},{2,6},{3,7},{4,0},{5,1},{6,2},{7,3},{8,12},{9,13},{10,... | collective-permute-start | bytes 49160 | tf_op jit(solution)/shard_map/ppermute | solution.py:180
  (32 other events, 780.9 us)

commit v2 on v1

--- a/solution.py
+++ b/solution.py
@@ -155,6 +155,42 @@
     return out
 
 
+def _grad_kernel(k, chunk, *refs):
+    a, b, out, bv, av, sems = refs[:k], refs[k:2 * k], refs[2 * k], refs[2 * k + 1], refs[2 * k + 2], refs[2 * k + 3]
+    r, rows = 0, []
+    for p in a:
+        rows.append((r, p.shape[0]))
+        r += p.shape[0]
+
+    @pl.when(pl.program_id(0) == 0)
+    def _():
+        copies = [pltpu.make_async_copy(b[j], bv.at[pl.ds(r, m), :], sems.at[j]) for j, (r, m) in enumerate(rows)]
+        for c in copies:
+            c.start()
+        for c in copies:
+            c.wait()
+
+    for j, (r, m) in enumerate(rows):
+        av[r:r + m, :] = a[j][...]
+
+    @pl.loop(0, out.shape[1] // chunk)
+    def _(i):
+        n = pl.multiple_of(i * chunk, chunk)
+        out[:, pl.ds(n, chunk)] = _tn(av[...], bv[:, pl.ds(n, chunk)])
+
+
+def _grad(a, b, tile, chunk):
+    k, rows, m, n = len(a), sum(p.shape[0] for p in a), a[0].shape[1], b[0].shape[1]
+    return pl.pallas_call(
+        functools.partial(_grad_kernel, k, chunk), grid=(m // tile,),
+        in_specs=[pl.BlockSpec((p.shape[0], tile), lambda i: (0, i)) for p in a] + [pl.BlockSpec(memory_space=pl.ANY)] * k,
+        out_specs=pl.BlockSpec((tile, n), lambda i: (i, 0)), out_shape=jax.ShapeDtypeStruct((m, n), F32),
+        scratch_shapes=[pltpu.VMEM((rows, n), BF), pltpu.VMEM((rows, tile), BF), pltpu.SemaphoreType.DMA((k,))],
+        compiler_params=pltpu.CompilerParams(vmem_limit_bytes=60 << 20, dimension_semantics=("arbitrary",)),
+        cost_estimate=pl.CostEstimate(flops=2 * rows * m * n, transcendentals=0, bytes_accessed=2 * rows * (m + n) + 4 * m * n),
+    )(*a, *b)
+
+
 def solution(mesh):
     rows = P(("data", "tp"), None)
     n = mesh.shape["tp"]
@@ -198,47 +234,50 @@
         g1d = send(g[0], down)
         g2u = send(g0u, up)
         g2d = send(g0d, down)
+        Hob, Yo, dAob, dXo, _ = step(lambda x, g, w, y, d: _pass("both", [w], xs=x, gs=g, y=y, d=d),
+                                     xn, g, (W1p, W2p), Yo, dXo)
         Gp0 = send(dY, swap)
         Xp0 = send(Xo, swap)
+        Hp0 = send(Hob[0], swap)
+        Dp0 = send(dAob[0], swap)
 
         ws = [(W1, W2), (W1p, W2p)]
-        Ae, He, Ye, (Xe,) = step(lambda x, w: _pass("fwd", w, xs=x), (x1d, x0d, x0u, x1u), ws)
-        Xp1 = send(Xe, swap)
-        Hp1 = send(He[1], swap)
         Af, Hf, Yf, (Xf,) = step(lambda x, w: _pass("fwd", w, xs=x), (x2u, x2d), ws)
         yfu = send(Yf[0], up)
         yfd = send(Yf[1], down)
+        Xp2 = send(Xf, swap)
+        Hp2 = send(Hf[1], swap)
+        Ae, He, Ye, (Xe,) = step(lambda x, w: _pass("fwd", w, xs=x), (x1d, x0d, x0u, x1u), ws)
         ypu = send(Ye[1], up)
         ypd = send(Ye[2], down)
-        Xp2 = send(Xf, swap)
-        Hp2 = send(Hf[1], swap)
-
-        dAr, dXr, (Gr,) = step(lambda g, w, a: _pass("bwd", w, gs=g, a=a),
-                               (g1d, g0d, g0u, g1u, g2u, g2d), ws, list(zip(Ae, Af)))
-        xfu = send(dXr[4], up)
-        xfd = send(dXr[5], down)
-        xpu = send(dXr[1], up)
-        xpd = send(dXr[2], down)
-        Dp1 = send(dAr[1], swap)
-        Gp1 = send(Gr, swap)
-
-        Hob, Yo, dAob, dXo, _ = step(lambda x, g, w, y, d: _pass("both", [w], xs=x, gs=g, y=y, d=d),
-                                     xn, g, (W1p, W2p), Yo, dXo)
-        Hp0 = send(Hob[0], swap)
-        Dp0 = send(dAob[0], swap)
-
-        dW1 = step(lambda a, b: _tn(cat(a), cat(b)), [Xo, Xe, Xf, Xp0, Xp1, Xp2], [dAoa[0], dAr[0], Dp0, Dp1])
+        Xp1 = send(Xe, swap)
+        Hp1 = send(He[1], swap)
+
+        def back(gs, a):
+            return step(lambda g, w, v: _pass("bwd", w, gs=g, a=v), gs, ws, [(v,) for v in a])
+
+        dAf, dXf, (Gf,) = back((g2u, g2d), Af)
+        xfu = send(dXf[0], up)
+        xfd = send(dXf[1], down)
+        Dp2 = send(dAf[1], swap)
+        Gp2 = send(Gf, swap)
+        dAe, dXe, (Ge,) = back((g1d, g0d, g0u, g1u), Ae)
+        xpu = send(dXe[1], up)
+        xpd = send(dXe[2], down)
+        Dp1 = send(dAe[1], swap)
+        Gp1 = send(Ge, swap)
+
+        Yt = step(lambda yo, u, d: X.astype(F32) + (cat(yo) + cat([d, u])), Yo, ypu, ypd)
 
         add2 = lambda a, b, u, d: (a + u, b + d)
-        xqu, xqd = step(add2, dXr[0], dXr[3], xfu, xfd)
+        xqu, xqd = step(add2, dXe[0], dXe[3], xfu, xfd)
         xqu = send(xqu, up)
         xqd = send(xqd, down)
         yqu, yqd = step(add2, Ye[0], Ye[3], yfu, yfd)
         yqu = send(yqu, up)
         yqd = send(yqd, down)
-        dW2 = step(lambda a, b: _tn(cat(a), cat(b)), [Hoa[0], He[0], Hf[0], Hp0, Hp1, Hp2], [dY, Gr, Gp0, Gp1])
-
-        Yt = step(lambda yo, u, d: X.astype(F32) + (cat(yo) + cat([d, u])), Yo, ypu, ypd)
+        dW1 = step(lambda a, b: _grad(a, b, 512, 896), [Xo, Xe, Xf, Xp0, Xp1, Xp2], [dAoa[0], dAe[0], dAf[0], Dp0, Dp1, Dp2])
+        dW2 = step(lambda a, b: _grad(a, b, 256, 1024), [Hoa[0], He[0], Hf[0], Hp0, Hp1, Hp2], [dY, Ge, Gf, Gp0, Gp1, Gp2])
 
         def fin(dxo, xpu, xqu, xpd, xqd):
             dXn = cat(dxo) + cat([xqu, xpu]) + cat([xpd, xqd])

time: 606 us -> 651 us (1.074)
  Pallas kernels: 201 us -> 302 us
  matrix products: 78 us -> 0 us
  waiting for transfers between devices: 246 us -> 265 us
  starting transfers between devices: 32.3 us -> 46.4 us
  local copies, waits for them, and re-layouts: 20.4 us -> 10 us
    pallas_call x0 -> x2, Pallas kernels: none -> 91.6 us  [_grad(): pl.pallas_call(functools.partial(_grad_kernel, k, chunk), grid=(m // tile...]
    dot_general x2 -> x0, matrix products: 78 us -> none  [_tn(): lax.dot_general(a, b, (((0,), (0,)), ((), ())), preferred_element_type=F32)]
    ppermute x40 -> x42, waiting for transfers between devices: 246 us -> 265 us  [send(): return lax.ppermute(v, 'tp', perm)]
    ppermute x40 -> x42, starting transfers between devices: 32.3 us -> 46.4 us  [send(): return lax.ppermute(v, 'tp', perm)]
    pallas_call x5 -> x6, Pallas kernels: 198 us -> 209 us  [_pass(): pl.pallas_call(functools.partial(_pass_kernel, mode, nx, nh, len(a[0]) if...]
    unnamed x58 -> x38, local copies, waits for them, and re-layouts: 15.7 us -> 6.84 us
  transfers between devices with their start and end apart: 40 -> 42, of which waited for: 13 -> 10; matrix products, arithmetic and copies ran while one was open for 19% -> 4% of each run, Pallas kernels for 33% -> 46%
where the time goes in v2:
time: 651 us; the launch traced here: 650 us
  Pallas kernels  302 us (46%)
  waiting for transfers between devices  265 us (41%)
  starting transfers between devices  46.4 us (7%)
  other arithmetic  26 us (4%)
  local copies, waits for them, and re-layouts  10 us (2%)
    ppermute x42, waiting for transfers between devices, send(): return lax.ppermute(v, 'tp', perm)  265 us
    pallas_call x6, Pallas kernels, _pass(): pl.pallas_call(functools.partial(_pass_kernel, mode, nx, nh, len(a[0]) if...  209 us
    pallas_call x2, Pallas kernels, _grad(): pl.pallas_call(functools.partial(_grad_kernel, k, chunk), grid=(m // tile...  91.6 us
    ppermute x42, starting transfers between devices, send(): return lax.ppermute(v, 'tp', perm)  46.4 us
  transfers between devices with their start and end apart: 42, of which 10 were waited for; matrix products, arithmetic and copies ran while one was open for 4% of the time, Pallas kernels for 46%

profile of v2, /device:TPU:112, one launch (start us, length us, event | category | flops | bytes accessed | tf_op | source)
XLA Modules:
  0.0 650.4 jit_solution(1514043729712775268)
XLA Ops:
  0.8 3.2 fusion.15
  12.1 21.5 %collective-permute-done.4.refs_2_ = bf16[128,4096]{1,0:T(8,128)(2,1)S(1)} collective-permute-done((bf16[128,4096]{1,0:T(8,128)(2,1)S(1)}, bf16[128,4096]{1,0:T(8,128)(2,1)S(1)}, u32[]{:S(2)}, u32[]{:S(2)}) %collective-permute-start.4) | collective-permute-done | bytes 1048608 | tf_op jit(solution)/shard_map/ppermute | solution.py:216
  34.7 26.6 %shard_map.92 = (bf16[256,1792]{1,0:T(8,128)(2,1)}, f32[128,4096]{1,0:T(8,128)}, f32[128,4096]{1,0:T(8,128)}, bf16[256,1792]{1,0:T(8,128)(2,1)}, f32[128,4096]{1...) custom-call(bf16[128,4096]{1,0:T(8,128)(2,1)} %copy-done.4, ...), custom_call_target="tpu_custom_call" | custom-call | flops 15032385536 | bytes 37748736 | tf_op jit(solution)/shard_map/pallas_call | solution.py:144
  61.3 3.1 collective-permute-start.2
  64.5 3.2 collective-permute-start.10
  67.7 3.2 collective-permute-start.7
  71.0 29.6 %shard_map.93 = (bf16[256,1792]{1,0:T(8,128)(2,1)}, f32[128,4096]{1,0:T(8,128)}, f32[128,4096]{1,0:T(8,128)}, bf16[256,1792]{1,0:T(8,128)(2,1)}, f32[128,4096]{1...) custom-call(bf16[128,4096]{1,0:T(8,128)(2,1)} %copy-done.4, ...), custom_call_target="tpu_custom_call" | custom-call | flops 15032385536 | bytes 37748736 | tf_op jit(solution)/shard_map/pallas_call | solution.py:144
  100.6 11.9 %collective-permute-done.6.refs_0_ = bf16[128,4096]{1,0:T(8,128)(2,1)S(1)} collective-permute-done((bf16[128,4096]{1,0:T(8,128)(2,1)}, bf16[128,4096]{1,0:T(8,128)(2,1)S(1)}, u32[]{:S(2)}, u32[]{:S(2)}) %collective-permute-start.6) | collective-permute-done | bytes 1048608 | tf_op jit(solution)/shard_map/ppermute | solution.py:216
  113.4 18.2 %collective-permute-done.7.refs_1_ = bf16[128,4096]{1,0:T(8,128)(2,1)} collective-permute-done((bf16[128,4096]{1,0:T(8,128)(2,1)}, bf16[128,4096]{1,0:T(8,128)(2,1)}, u32[]{:S(2)}, u32[]{:S(2)}) %collective-permute-start.7) | collective-permute-done | bytes 1048608 | tf_op jit(solution)/shard_map/ppermute | solution.py:216
  132.5 29.3 %shard_map.94 = (f32[256,1792]{1,0:T(8,128)}, f32[256,1792]{1,0:T(8,128)}, bf16[256,1792]{1,0:T(8,128)(2,1)}, bf16[256,1792]{1,0:T(8,128)(2,1)}, f32[128,4096]{1...) custom-call(bf16[128,4096]{1,0:T(8,128)(2,1)} %copy-done.12, ...), custom_call_target="tpu_custom_call" | custom-call | flops 15032385536 | bytes 67108864 | tf_op jit(solution)/shard_map/pallas_call | solution.py:144
  161.8 2.9 collective-permute-start.15
  164.6 45.1 %shard_map.95 = (f32[512,1792]{1,0:T(8,128)}, f32[512,1792]{1,0:T(8,128)}, bf16[512,1792]{1,0:T(8,128)(2,1)}, bf16[512,1792]{1,0:T(8,128)(2,1)}, f32[128,4096]{1...) custom-call(bf16[128,4096]{1,0:T(8,128)(2,1)} %collective-permute-done, ...), custom_call_target="tpu_custom_call" | custom-call | flops 30064771072 | bytes 75497472 | tf_op jit(solution)/shard_map/pallas_call | solution.py:144
  210.8 30.7 %shard_map.96 = (bf16[256,1792]{1,0:T(8,128)(2,1)}, bf16[256,1792]{1,0:T(8,128)(2,1)}, f32[128,4096]{1,0:T(8,128)}, f32[128,4096]{1,0:T(8,128)}, bf16[256,4096]{1,0:T(8,128)(2,1)}) custom-call(bf16[128,4096]{1,0:T(8,128)(2,1)} %copy-done.11, bf16[128,4096]{1,0:T(8,128)(2,1)} %collective-permute-done.15.refs_1_, bf16[4096,1792]{1,0:T(8,128)(2,1)} %refs_4_.4, ...), custom_call_target="tpu_custom_call" | custom-call | flops 15032385536 | bytes 67108864 | tf_op jit(solution)/shard_map/pallas_call | solution.py:144
  241.7 47.3 %shard_map.97 = (bf16[512,1792]{1,0:T(8,128)(2,1)}, bf16[512,1792]{1,0:T(8,128)(2,1)}, f32[128,4096]{1,0:T(8,128)}, f32[128,4096]{1,0:T(8,128)}, f32[128,4096]{1...) custom-call(bf16[128,4096]{1,0:T(8,128)(2,1)} %collective-permute-done.10.refs_0_, ...), custom_call_target="tpu_custom_call" | custom-call | flops 30064771072 | bytes 75497472 | tf_op jit(solution)/shard_map/pallas_call | solution.py:144
  289.6 3.2 collective-permute-start.9
  292.9 2.8 collective-permute-done.37.refs_11_
  295.7 3.2 collective-permute-start.17
  298.9 40.6 %collective-permute-done.8 = f32[128,4096]{1,0:T(8,128)S(1)} collective-permute-done((f32[128,4096]{1,0:T(8,128)}, f32[128,4096]{1,0:T(8,128)S(1)}, u32[]{:S(2)}, u32[]{:S(2)}) %collective-permute-start.8) | collective-permute-done | bytes 2097184 | tf_op jit(solution)/shard_map/ppermute | solution.py:216
  339.5 3.2 collective-permute-start.19
  342.7 41.7 %collective-permute-done.16 = f32[128,4096]{1,0:T(8,128)S(1)} collective-permute-done((f32[128,4096]{1,0:T(8,128)}, f32[128,4096]{1,0:T(8,128)S(1)}, u32[]{:S(2)}, u32[]{:S(2)}) %collective-permute-start.16) | collective-permute-done | bytes 2097184 | tf_op jit(solution)/shard_map/ppermute | solution.py:216
  384.9 43.6 %collective-permute-done.18 = f32[128,4096]{1,0:T(8,128)S(1)} collective-permute-done((f32[128,4096]{1,0:T(8,128)}, f32[128,4096]{1,0:T(8,128)S(1)}, u32[]{:S(2)}, u32[]{:S(2)}) %collective-permute-start.18) | collective-permute-done | bytes 2097184 | tf_op jit(solution)/shard_map/ppermute | solution.py:216
  430.8 3.8 fusion.11
  444.4 45.9 %shard_map.98 = f32[4096,1792]{1,0:T(8,128)} custom-call(bf16[256,4096]{1,0:T(8,128)(2,1)} %get-tuple-element.322.refs_0_, bf16[512,4096]{1,0:T(8,128)(2,1)} %get-tuple-element.323.refs_1_, bf16[256,4096]{1,0:T(8,128)(2,1)} %get-tuple-element.324.refs_2_, bf16[256,4096]{1,0:T(8,128)(2,1)} %copy-done.13, bf16[512,4096]{1,0:T(8,128)(2,1)} %collective-permute-done.33.refs_4_, ...), custom_call_target="tpu_custom_call" | custom-call | flops 30064771072 | bytes 53477376 | tf_op jit(solution)/shard_map/pallas_call | solution.py:184
  490.3 2.9 collective-permute-start.24
  493.2 3.2 collective-permute-start.21
  496.5 3.2 collective-permute-start.25
  499.7 45.6 %shard_map.99 = f32[1792,4096]{1,0:T(8,128)} custom-call(bf16[256,1792]{1,0:T(8,128)(2,1)} %get-tuple-element.334.refs_0_, bf16[512,1792]{1,0:T(8,128)(2,1)} %get-tuple-element.335.refs_1_, bf16[256,1792]{1,0:T(8,128)(2,1)} %get-tuple-element.336.refs_2_, bf16[256,1792]{1,0:T(8,128)(2,1)} %collective-permute-done.26.refs_3_, ...), custom_call_target="tpu_custom_call" | custom-call | flops 30064771072 | bytes 53477376 | tf_op jit(solution)/shard_map/pallas_call | solution.py:184
  545.4 42.0 %collective-permute-done.23 = f32[128,4096]{1,0:T(8,128)} collective-permute-done((f32[128,4096]{1,0:T(8,128)}, f32[128,4096]{1,0:T(8,128)}, u32[]{:S(2)}, u32[]{:S(2)}) %collective-permute-start.23) | collective-permute-done | bytes 2097184 | tf_op jit(solution)/shard_map/ppermute | solution.py:216
  587.4 41.5 %collective-permute-done.25 = f32[128,4096]{1,0:T(8,128)} collective-permute-done((f32[128,4096]{1,0:T(8,128)}, f32[128,4096]{1,0:T(8,128)}, u32[]{:S(2)}, u32[]{:S(2)}) %collective-permute-start.25) | collective-permute-done | bytes 2097184 | tf_op jit(solution)/shard_map/ppermute | solution.py:216
  628.9 5.6 fusion.6
  634.5 5.1 fusion.10
  645.7 4.1 fusion.13
  (114 shorter events, 32.2 us)
Async XLA Ops:
  0.7 67.1 %collective-permute-start = (bf16[4096,1792]{1,0:T(8,128)(2,1)}, bf16[4096,1792]{1,0:T(8,128)(2,1)}, u32[]{:S(2)}, u32[]{:S(2)}) collective-permute-start(bf16[4096,1792]{1,0:T(8,128)(2,1)} %refs_4_.4), channel_id=1, source_target_pairs={{0,1},{1,0},{2,3},{3,2},{4,5},{5,4},{6,7},{7,6},{8,9},{9,8},{10,11... | collective-permute-start | bytes 44040200 | tf_op jit(solution)/shard_map/ppermute | solution.py:216
  5.7 62.0 %collective-permute-start.1 = (bf16[1792,4096]{1,0:T(8,128)(2,1)}, bf16[1792,4096]{1,0:T(8,128)(2,1)}, u32[]{:S(2)}, u32[]{:S(2)}) collective-permute-start(bf16[1792,4096]{1,0:T(8,128)(2,1)} %refs_6_.1), channel_id=1, source_target_pairs={{0,1},{1,0},{2,3},{3,2},{4,5},{5,4},{6,7},{7,6},{8,9},{9,8},{10,11... | collective-permute-start | bytes 44040200 | tf_op jit(solution)/shard_map/ppermute | solution.py:216
  8.5 52.8 %collective-permute-start.3 = (bf16[128,4096]{1,0:T(8,128)(2,1)S(1)}, bf16[128,4096]{1,0:T(8,128)(2,1)}, u32[]{:S(2)}, u32[]{:S(2)}) collective-permute-start(bf16[128,4096]{1,0:T(8,128)(2,1)S(1)} %get-tuple-element.211.refs_1_), channel_id=1, source_target_pairs={{0,6},{1,7},{2,0},{3,1},{4,2},{5,3},{6,4},{7,5},{8,14},{9,15},{10,... | collective-permute-start | bytes 3145736 | tf_op jit(solution)/shard_map/ppermute | solution.py:216
  10.6 53.9 %collective-permute-start.11 = (bf16[128,4096]{1,0:T(8,128)(2,1)}, bf16[128,4096]{1,0:T(8,128)(2,1)}, u32[]{:S(2)}, u32[]{:S(2)}) collective-permute-start(bf16[128,4096]{1,0:T(8,128)(2,1)} %get-tuple-element.236), channel_id=1, source_target_pairs={{0,6},{1,7},{2,0},{3,1},{4,2},{5,3},{6,4},{7,5},{8,14},{9,15},{10,... | collective-permute-start | bytes 3145736 | tf_op jit(solution)/shard_map/ppermute | solution.py:216
  61.3 100.4 %collective-permute-start.2 = (bf16[128,4096]{1,0:T(8,128)(2,1)}, bf16[128,4096]{1,0:T(8,128)(2,1)}, u32[]{:S(2)}, u32[]{:S(2)}) collective-permute-start(bf16[128,4096]{1,0:T(8,128)(2,1)} %copy-done.4), channel_id=1, source_target_pairs={{0,6},{1,7},{2,0},{3,1},{4,2},{5,3},{6,4},{7,5},{8,14},{9,15},{10,... | collective-permute-start | bytes 3145736 | tf_op jit(solution)/shard_map/ppermute | solution.py:216
  64.5 100.2 %collective-permute-start.5 = (bf16[128,4096]{1,0:T(8,128)(2,1)}, bf16[128,4096]{1,0:T(8,128)(2,1)}, u32[]{:S(2)}, u32[]{:S(2)}) collective-permute-start(bf16[128,4096]{1,0:T(8,128)(2,1)} %copy-done.3), channel_id=1, source_target_pairs={{0,2},{1,3},{2,4},{3,5},{4,6},{5,7},{6,0},{7,1},{8,10},{9,11},{10,... | collective-permute-start | bytes 3145736 | tf_op jit(solution)/shard_map/ppermute | solution.py:216
  64.5 177.1 %collective-permute-start.10 = (bf16[128,4096]{1,0:T(8,128)(2,1)}, bf16[128,4096]{1,0:T(8,128)(2,1)}, u32[]{:S(2)}, u32[]{:S(2)}) collective-permute-start(bf16[128,4096]{1,0:T(8,128)(2,1)} %get-tuple-element.237.refs_2_), channel_id=1, source_target_pairs={{0,6},{1,7},{2,0},{3,1},{4,2},{5,3},{6,4},{7,5},{8,14},{9,15},{10,... | collective-permute-start | bytes 3145736 | tf_op jit(solution)/shard_map/ppermute | solution.py:216
  67.7 44.7 %collective-permute-start.6 = (bf16[128,4096]{1,0:T(8,128)(2,1)}, bf16[128,4096]{1,0:T(8,128)(2,1)S(1)}, u32[]{:S(2)}, u32[]{:S(2)}) collective-permute-start(bf16[128,4096]{1,0:T(8,128)(2,1)} %copy-done.16), channel_id=1, source_target_pairs={{0,2},{1,3},{2,4},{3,5},{4,6},{5,7},{6,0},{7,1},{8,10},{9,11},{10,... | collective-permute-start | bytes 3145736 | tf_op jit(solution)/shard_map/ppermute | solution.py:216
  67.7 63.9 %collective-permute-start.7 = (bf16[128,4096]{1,0:T(8,128)(2,1)}, bf16[128,4096]{1,0:T(8,128)(2,1)}, u32[]{:S(2)}, u32[]{:S(2)}) collective-permute-start(bf16[128,4096]{1,0:T(8,128)(2,1)} %collective-permute-done.3.refs_1_), channel_id=1, source_target_pairs={{0,6},{1,7},{2,0},{3,1},{4,2},{5,3},{6,4},{7,5},{8,14},{9,15},{10,... | collective-permute-start | bytes 3145736 | tf_op jit(solution)/shard_map/ppermute | solution.py:216
  112.4 129.1 %collective-permute-start.13 = (bf16[128,4096]{1,0:T(8,128)(2,1)}, bf16[128,4096]{1,0:T(8,128)(2,1)}, u32[]{:S(2)}, u32[]{:S(2)}) collective-permute-start(bf16[128,4096]{1,0:T(8,128)(2,1)} %get-tuple-element.238.refs_3_), channel_id=1, source_target_pairs={{0,2},{1,3},{2,4},{3,5},{4,6},{5,7},{6,0},{7,1},{8,10},{9,11},{10,... | collective-permute-start | bytes 3145736 | tf_op jit(solution)/shard_map/ppermute | solution.py:216
  131.6 78.2 %collective-permute-start.14 = (bf16[128,4096]{1,0:T(8,128)(2,1)}, bf16[128,4096]{1,0:T(8,128)(2,1)S(1)}, u32[]{:S(2)}, u32[]{:S(2)}) collective-permute-start(bf16[128,4096]{1,0:T(8,128)(2,1)} %collective-permute-done.12.refs_2_), channel_id=1, source_target_pairs={{0,2},{1,3},{2,4},{3,5},{4,6},{5,7},{6,0},{7,1},{8,10},{9,11},{10,... | collective-permute-start | bytes 3145736 | tf_op jit(solution)/shard_map/ppermute | solution.py:216
  161.8 48.0 %collective-permute-start.15 = (bf16[128,4096]{1,0:T(8,128)(2,1)}, bf16[128,4096]{1,0:T(8,128)(2,1)}, u32[]{:S(2)}, u32[]{:S(2)}) collective-permute-start(bf16[128,4096]{1,0:T(8,128)(2,1)} %collective-permute-done.11.refs_1_), channel_id=1, source_target_pairs={{0,6},{1,7},{2,0},{3,1},{4,2},{5,3},{6,4},{7,5},{8,14},{9,15},{10,... | collective-permute-start | bytes 3145736 | tf_op jit(solution)/shard_map/ppermute | solution.py:216
  241.6 51.3 %collective-permute-start.35 = (bf16[256,1792]{1,0:T(8,128)(2,1)S(1)}, bf16[256,1792]{1,0:T(8,128)(2,1)S(1)}, u32[]{:S(2)}, u32[]{:S(2)}) collective-permute-start(bf16[256,1792]{1,0:T(8,128)(2,1)S(1)} %copy-done.18), channel_id=1, source_target_pairs={{0,1},{1,0},{2,3},{3,2},{4,5},{5,4},{6,7},{7,6},{8,9},{9,8},{10,11... | collective-permute-start | bytes 2752520 | tf_op jit(solution)/shard_map/ppermute | solution.py:216
  289.6 49.9 %collective-permute-start.8 = (f32[128,4096]{1,0:T(8,128)}, f32[128,4096]{1,0:T(8,128)S(1)}, u32[]{:S(2)}, u32[]{:S(2)}) collective-permute-start(f32[128,4096]{1,0:T(8,128)} %get-tuple-element.232), channel_id=1, source_target_pairs={{0,2},{1,3},{2,4},{3,5},{4,6},{5,7},{6,0},{7,1},{8,10},{9,11},{10,... | collective-permute-start | bytes 6291464 | tf_op jit(solution)/shard_map/ppermute | solution.py:216
  289.6 49.9 %collective-permute-start.9 = (f32[128,4096]{1,0:T(8,128)}, f32[128,4096]{1,0:T(8,128)S(1)}, u32[]{:S(2)}, u32[]{:S(2)}) collective-permute-start(f32[128,4096]{1,0:T(8,128)} %get-tuple-element.234), channel_id=1, source_target_pairs={{0,6},{1,7},{2,0},{3,1},{4,2},{5,3},{6,4},{7,5},{8,14},{9,15},{10,... | collective-permute-start | bytes 6291464 | tf_op jit(solution)/shard_map/ppermute | solution.py:216
  292.8 91.6 %collective-permute-start.16 = (f32[128,4096]{1,0:T(8,128)}, f32[128,4096]{1,0:T(8,128)S(1)}, u32[]{:S(2)}, u32[]{:S(2)}) collective-permute-start(f32[128,4096]{1,0:T(8,128)} %get-tuple-element.270), channel_id=1, source_target_pairs={{0,2},{1,3},{2,4},{3,5},{4,6},{5,7},{6,0},{7,1},{8,10},{9,11},{10,... | collective-permute-start | bytes 6291464 | tf_op jit(solution)/shard_map/ppermute | solution.py:216
  295.7 88.7 %collective-permute-start.17 = (f32[128,4096]{1,0:T(8,128)}, f32[128,4096]{1,0:T(8,128)S(1)}, u32[]{:S(2)}, u32[]{:S(2)}) collective-permute-start(f32[128,4096]{1,0:T(8,128)} %get-tuple-element.272), channel_id=1, source_target_pairs={{0,6},{1,7},{2,0},{3,1},{4,2},{5,3},{6,4},{7,5},{8,14},{9,15},{10,... | collective-permute-start | bytes 6291464 | tf_op jit(solution)/shard_map/ppermute | solution.py:216
  298.9 144.5 %collective-permute-start.33 = (bf16[512,4096]{1,0:T(8,128)(2,1)}, bf16[512,4096]{1,0:T(8,128)(2,1)}, u32[]{:S(2)}, u32[]{:S(2)}) collective-permute-start(bf16[512,4096]{1,0:T(8,128)(2,1)} %get-tuple-element.323.refs_1_), channel_id=1, source_target_pairs={{0,1},{1,0},{2,3},{3,2},{4,5},{5,4},{6,7},{7,6},{8,9},{9,8},{10,11... | collective-permute-start | bytes 12582920 | tf_op jit(solution)/shard_map/ppermute | solution.py:216
  339.5 89.0 %collective-permute-start.18 = (f32[128,4096]{1,0:T(8,128)}, f32[128,4096]{1,0:T(8,128)S(1)}, u32[]{:S(2)}, u32[]{:S(2)}) collective-permute-start(f32[128,4096]{1,0:T(8,128)} %get-tuple-element.276), channel_id=1, source_target_pairs={{0,2},{1,3},{2,4},{3,5},{4,6},{5,7},{6,0},{7,1},{8,10},{9,11},{10,... | collective-permute-start | bytes 6291464 | tf_op jit(solution)/shard_map/ppermute | solution.py:216
  339.5 89.4 %collective-permute-start.19 = (f32[128,4096]{1,0:T(8,128)}, f32[128,4096]{1,0:T(8,128)S(1)}, u32[]{:S(2)}, u32[]{:S(2)}) collective-permute-start(f32[128,4096]{1,0:T(8,128)} %get-tuple-element.278), channel_id=1, source_target_pairs={{0,6},{1,7},{2,0},{3,1},{4,2},{5,3},{6,4},{7,5},{8,14},{9,15},{10,... | collective-permute-start | bytes 6291464 | tf_op jit(solution)/shard_map/ppermute | solution.py:216
  384.4 45.0 %collective-permute-start.32 = (bf16[256,4096]{1,0:T(8,128)(2,1)}, bf16[256,4096]{1,0:T(8,128)(2,1)S(1)}, u32[]{:S(2)}, u32[]{:S(2)}) collective-permute-start(bf16[256,4096]{1,0:T(8,128)(2,1)} %get-tuple-element.322.refs_0_), channel_id=1, source_target_pairs={{0,1},{1,0},{2,3},{3,2},{4,5},{5,4},{6,7},{7,6},{8,9},{9,8},{10,11... | collective-permute-start | bytes 6291464 | tf_op jit(solution)/shard_map/ppermute | solution.py:216
  384.4 58.9 %collective-permute-start.34 = (bf16[256,4096]{1,0:T(8,128)(2,1)}, bf16[256,4096]{1,0:T(8,128)(2,1)}, u32[]{:S(2)}, u32[]{:S(2)}) collective-permute-start(bf16[256,4096]{1,0:T(8,128)(2,1)} %get-tuple-element.324.refs_2_), channel_id=1, source_target_pairs={{0,1},{1,0},{2,3},{3,2},{4,5},{5,4},{6,7},{7,6},{8,9},{9,8},{10,11... | collective-permute-start | bytes 6291464 | tf_op jit(solution)/shard_map/ppermute | solution.py:216
  428.5 68.0 %collective-permute-start.30 = (bf16[512,4096]{1,0:T(8,128)(2,1)}, bf16[512,4096]{1,0:T(8,128)(2,1)}, u32[]{:S(2)}, u32[]{:S(2)}) collective-permute-start(bf16[512,4096]{1,0:T(8,128)(2,1)} %get-tuple-element.341.refs_7_), channel_id=1, source_target_pairs={{0,1},{1,0},{2,3},{3,2},{4,5},{5,4},{6,7},{7,6},{8,9},{9,8},{10,11... | collective-permute-start | bytes 12582920 | tf_op jit(solution)/shard_map/ppermute | solution.py:216
  443.3 53.1 %collective-permute-start.22 = (f32[128,4096]{1,0:T(8,128)}, f32[128,4096]{1,0:T(8,128)}, u32[]{:S(2)}, u32[]{:S(2)}) collective-permute-start(f32[128,4096]{1,0:T(8,128)} %get-tuple-element.290), channel_id=1, source_target_pairs={{0,2},{1,3},{2,4},{3,5},{4,6},{5,7},{6,0},{7,1},{8,10},{9,11},{10,... | collective-permute-start | bytes 6291464 | tf_op jit(solution)/shard_map/ppermute | solution.py:216
  443.8 46.5 %collective-permute-start.27 = (bf16[512,1792]{1,0:T(8,128)(2,1)S(1)}, bf16[512,1792]{1,0:T(8,128)(2,1)}, u32[]{:S(2)}, u32[]{:S(2)}) collective-permute-start(bf16[512,1792]{1,0:T(8,128)(2,1)S(1)} %copy-done.14), channel_id=1, source_target_pairs={{0,1},{1,0},{2,3},{3,2},{4,5},{5,4},{6,7},{7,6},{8,9},{9,8},{10,11... | collective-permute-start | bytes 5505032 | tf_op jit(solution)/shard_map/ppermute | solution.py:216
  443.8 49.4 %collective-permute-start.29 = (bf16[256,4096]{1,0:T(8,128)(2,1)}, bf16[256,4096]{1,0:T(8,128)(2,1)}, u32[]{:S(2)}, u32[]{:S(2)}) collective-permute-start(bf16[256,4096]{1,0:T(8,128)(2,1)} %refs_6_.2), channel_id=1, source_target_pairs={{0,1},{1,0},{2,3},{3,2},{4,5},{5,4},{6,7},{7,6},{8,9},{9,8},{10,11... | collective-permute-start | bytes 6291464 | tf_op jit(solution)/shard_map/ppermute | solution.py:216
  444.3 48.9 %collective-permute-start.31 = (bf16[256,4096]{1,0:T(8,128)(2,1)}, bf16[256,4096]{1,0:T(8,128)(2,1)}, u32[]{:S(2)}, u32[]{:S(2)}) collective-permute-start(bf16[256,4096]{1,0:T(8,128)(2,1)} %get-tuple-element.342.refs_8_), channel_id=1, source_target_pairs={{0,1},{1,0},{2,3},{3,2},{4,5},{5,4},{6,7},{7,6},{8,9},{9,8},{10,11... | collective-permute-start | bytes 6291464 | tf_op jit(solution)/shard_map/ppermute | solution.py:216
  490.3 55.0 %collective-permute-start.24 = (f32[128,4096]{1,0:T(8,128)}, f32[128,4096]{1,0:T(8,128)}, u32[]{:S(2)}, u32[]{:S(2)}) collective-permute-start(f32[128,4096]{1,0:T(8,128)} %get-tuple-element.293), channel_id=1, source_target_pairs={{0,6},{1,7},{2,0},{3,1},{4,2},{5,3},{6,4},{7,5},{8,14},{9,15},{10,... | collective-permute-start | bytes 6291464 | tf_op jit(solution)/shard_map/ppermute | solution.py:216
  493.2 152.4 %collective-permute-start.20 = (f32[128,4096]{1,0:T(8,128)}, f32[128,4096]{1,0:T(8,128)}, u32[]{:S(2)}, u32[]{:S(2)}) collective-permute-start(f32[128,4096]{1,0:T(8,128)} %add.56), channel_id=1, source_target_pairs={{0,2},{1,3},{2,4},{3,5},{4,6},{5,7},{6,0},{7,1},{8,10},{9,11},{10,... | collective-permute-start | bytes 6291464 | tf_op jit(solution)/shard_map/ppermute | solution.py:216
  493.2 152.4 %collective-permute-start.21 = (f32[128,4096]{1,0:T(8,128)}, f32[128,4096]{1,0:T(8,128)}, u32[]{:S(2)}, u32[]{:S(2)}) collective-permute-start(f32[128,4096]{1,0:T(8,128)} %add.57), channel_id=1, source_target_pairs={{0,6},{1,7},{2,0},{3,1},{4,2},{5,3},{6,4},{7,5},{8,14},{9,15},{10,... | collective-permute-start | bytes 6291464 | tf_op jit(solution)/shard_map/ppermute | solution.py:216
  496.5 90.9 %collective-permute-start.23 = (f32[128,4096]{1,0:T(8,128)}, f32[128,4096]{1,0:T(8,128)}, u32[]{:S(2)}, u32[]{:S(2)}) collective-permute-start(f32[128,4096]{1,0:T(8,128)} %add.55), channel_id=1, source_target_pairs={{0,2},{1,3},{2,4},{3,5},{4,6},{5,7},{6,0},{7,1},{8,10},{9,11},{10,... | collective-permute-start | bytes 6291464 | tf_op jit(solution)/shard_map/ppermute | solution.py:216
  496.5 132.4 %collective-permute-start.25 = (f32[128,4096]{1,0:T(8,128)}, f32[128,4096]{1,0:T(8,128)}, u32[]{:S(2)}, u32[]{:S(2)}) collective-permute-start(f32[128,4096]{1,0:T(8,128)} %add.58), channel_id=1, source_target_pairs={{0,6},{1,7},{2,0},{3,1},{4,2},{5,3},{6,4},{7,5},{8,14},{9,15},{10,... | collective-permute-start | bytes 6291464 | tf_op jit(solution)/shard_map/ppermute | solution.py:216
  (29 other events, 670.1 us)

commit v3 on v2

--- a/solution.py
+++ b/solution.py
@@ -41,6 +41,40 @@
     gamma = gamma_ref[...]
     for out, r in ((top_ref, 0), (bot_ref, h)):
         out[...] = (_ln(x_ref[r:r + h, :].astype(F32))[0] * gamma).astype(BF)
+
+
+STEP = 32
+
+
+def _last_kernel(k, t_ref, u_ref, d_ref, *refs):
+    i = pl.program_id(0)
+
+    @pl.when(i < k)
+    def _():
+        refs[-1][...] = (t_ref[...] + u_ref[...]).astype(BF)
+
+    @pl.when(i >= k)
+    def _():
+        refs[-1][...] = (t_ref[...] + d_ref[...]).astype(BF)
+
+
+def _last(t, u, d, y=None):
+    rows, dm = t.shape
+    half, k = rows // 2 // STEP, u.shape[0] // STEP
+    off = 0 if y is None else half - 1
+
+    def block(f):
+        return pl.BlockSpec((STEP, dm), lambda i: (f(i), 0))
+
+    place = block(lambda i: off + jnp.where(i < k, i, i - k + half))
+    return pl.pallas_call(
+        functools.partial(_last_kernel, k), grid=(2 * k,), out_shape=jax.ShapeDtypeStruct((rows, dm), BF),
+        in_specs=[place, block(lambda i: jnp.minimum(i, k - 1)), block(lambda i: jnp.maximum(i - k, 0))]
+        + ([] if y is None else [pl.BlockSpec(memory_space=pl.ANY)]),
+        out_specs=place, input_output_aliases={} if y is None else {3: 0},
+        compiler_params=pltpu.CompilerParams(dimension_semantics=("arbitrary",)),
+        cost_estimate=pl.CostEstimate(flops=4 * u.size, bytes_accessed=20 * u.size, transcendentals=0),
+    )(t, u, d, *(() if y is None else (y,)))
 
 
 def _norm(x, gamma):
@@ -270,12 +304,16 @@
         Yt = step(lambda yo, u, d: X.astype(F32) + (cat(yo) + cat([d, u])), Yo, ypu, ypd)
 
         add2 = lambda a, b, u, d: (a + u, b + d)
+        m = h - STEP
+        yq = step(lambda a, b, u, d: (a[:m] + u[:m], b[:m] + d[:m], a[m:] + u[m:], b[m:] + d[m:]), Ye[0], Ye[3], yfu, yfd)
         xqu, xqd = step(add2, dXe[0], dXe[3], xfu, xfd)
         xqu = send(xqu, up)
         xqd = send(xqd, down)
-        yqu, yqd = step(add2, Ye[0], Ye[3], yfu, yfd)
-        yqu = send(yqu, up)
-        yqd = send(yqd, down)
+        yqu = send(yq[0], up)
+        yqd = send(yq[1], down)
+        yru = send(yq[2], up)
+        yrd = send(yq[3], down)
+
         dW1 = step(lambda a, b: _grad(a, b, 512, 896), [Xo, Xe, Xf, Xp0, Xp1, Xp2], [dAoa[0], dAe[0], dAf[0], Dp0, Dp1, Dp2])
         dW2 = step(lambda a, b: _grad(a, b, 256, 1024), [Hoa[0], He[0], Hf[0], Hp0, Hp1, Hp2], [dY, Ge, Gf, Gp0, Gp1, Gp2])
 
@@ -291,7 +329,8 @@
         dgam = step(lambda a, b: a + b, dgam, send(dgam, swap))
         dgs = send(dgam, up), send(dgam, down), send(dgam, over)
 
-        Y = step(lambda t, u, d: (t + cat([u, d])).astype(BF), Yt, yqu, yqd)
+        Y = step(lambda *v: _last(*v), Yt, yqu, yqd)
+        Y = step(lambda *v: _last(*v), Yt, yru, yrd, Y)
         dgam = dgam + dgs[0] + dgs[1] + dgs[2]
         return Y, dX, dW1, dW2, dgam[0]
 

time: 651 us -> 603 us (0.926)
  waiting for transfers between devices: 265 us -> 216 us
  starting transfers between devices: 46.4 us -> 35.8 us
  Pallas kernels: 302 us -> 310 us
    ppermute x42 -> x44, waiting for transfers between devices: 265 us -> 216 us  [send(): return lax.ppermute(v, 'tp', perm)]
    ppermute x42 -> x44, starting transfers between devices: 46.4 us -> 35.8 us  [send(): return lax.ppermute(v, 'tp', perm)]
    pallas_call x0 -> x2, Pallas kernels: none -> 7.95 us  [_last(): pl.pallas_call(functools.partial(_last_kernel, k), grid=(2 * k,), out_sha...]
    add x0 -> x3, other arithmetic: none -> 7.7 us  [the longest x1 3.53 us: body(): b[:m] + d[:m]]
  transfers between devices with their start and end apart: 42 -> 44, of which waited for: 10 -> 10; matrix products, arithmetic and copies ran while one was open for 4% -> 6% of each run, Pallas kernels for 46% -> 51%
where the time goes in v3:
time: 603 us
  Pallas kernels  310 us (51%)
  waiting for transfers between devices  216 us (36%)
  starting transfers between devices  35.8 us (6%)
  other arithmetic  31.6 us (5%)
  local copies, waits for them, and re-layouts  8.7 us (1%)
    ppermute x44, waiting for transfers between devices, send(): return lax.ppermute(v, 'tp', perm)  216 us
    pallas_call x6, Pallas kernels, _pass(): pl.pallas_call(functools.partial(_pass_kernel, mode, nx, nh, len(a[0]) if...  209 us
    pallas_call x2, Pallas kernels, _grad(): pl.pallas_call(functools.partial(_grad_kernel, k, chunk), grid=(m // tile...  91.6 us
    ppermute x44, starting transfers between devices, send(): return lax.ppermute(v, 'tp', perm)  35.8 us
  transfers between devices with their start and end apart: 44, of which 10 were waited for; matrix products, arithmetic and copies ran while one was open for 6% of the time, Pallas kernels for 51%

profile of v3, /device:TPU:112, one launch (start us, length us, event | category | flops | bytes accessed | tf_op | source)
XLA Modules:
  0.0 603.0 jit_solution(4304301761244774109)
XLA Ops:
  0.8 3.2 fusion.14
  6.2 2.3 collective-permute-start.4
  12.1 21.5 %collective-permute-done.4.refs_2_ = bf16[128,4096]{1,0:T(8,128)(2,1)S(1)} collective-permute-done((bf16[128,4096]{1,0:T(8,128)(2,1)S(1)}, bf16[128,4096]{1,0:T(8,128)(2,1)S(1)}, u32[]{:S(2)}, u32[]{:S(2)}) %collective-permute-start.4) | collective-permute-done | bytes 1048608 | tf_op jit(solution)/shard_map/ppermute | solution.py:250
  34.8 26.6 %shard_map.92 = (bf16[256,1792]{1,0:T(8,128)(2,1)}, f32[128,4096]{1,0:T(8,128)}, f32[128,4096]{1,0:T(8,128)}, bf16[256,1792]{1,0:T(8,128)(2,1)}, f32[128,4096]{1...) custom-call(bf16[128,4096]{1,0:T(8,128)(2,1)} %copy-done.4, ...), custom_call_target="tpu_custom_call" | custom-call | flops 15032385536 | bytes 37748736 | tf_op jit(solution)/shard_map/pallas_call | solution.py:178
  61.3 3.1 collective-permute-start.2
  65.1 2.7 collective-permute-start.7
  67.8 29.6 %shard_map.93 = (bf16[256,1792]{1,0:T(8,128)(2,1)}, f32[128,4096]{1,0:T(8,128)}, f32[128,4096]{1,0:T(8,128)}, bf16[256,1792]{1,0:T(8,128)(2,1)}, f32[128,4096]{1...) custom-call(bf16[128,4096]{1,0:T(8,128)(2,1)} %copy-done.4, ...), custom_call_target="tpu_custom_call" | custom-call | flops 15032385536 | bytes 37748736 | tf_op jit(solution)/shard_map/pallas_call | solution.py:178
  97.4 17.1 %collective-permute-done.6.refs_0_ = bf16[128,4096]{1,0:T(8,128)(2,1)} collective-permute-done((bf16[128,4096]{1,0:T(8,128)(2,1)}, bf16[128,4096]{1,0:T(8,128)(2,1)}, u32[]{:S(2)}, u32[]{:S(2)}) %collective-permute-start.6) | collective-permute-done | bytes 1048608 | tf_op jit(solution)/shard_map/ppermute | solution.py:250
  114.5 29.2 %shard_map.94 = (f32[256,1792]{1,0:T(8,128)}, f32[256,1792]{1,0:T(8,128)}, bf16[256,1792]{1,0:T(8,128)(2,1)}, bf16[256,1792]{1,0:T(8,128)(2,1)}, f32[128,4096]{1...) custom-call(bf16[128,4096]{1,0:T(8,128)(2,1)} %collective-permute-done.6.refs_0_, ...), custom_call_target="tpu_custom_call" | custom-call | flops 15032385536 | bytes 67108864 | tf_op jit(solution)/shard_map/pallas_call | solution.py:178
  143.7 45.1 %shard_map.95 = (f32[512,1792]{1,0:T(8,128)}, f32[512,1792]{1,0:T(8,128)}, bf16[512,1792]{1,0:T(8,128)(2,1)}, bf16[512,1792]{1,0:T(8,128)(2,1)}, f32[128,4096]{1...) custom-call(bf16[128,4096]{1,0:T(8,128)(2,1)} %collective-permute-done, ...), custom_call_target="tpu_custom_call" | custom-call | flops 30064771072 | bytes 75497472 | tf_op jit(solution)/shard_map/pallas_call | solution.py:178
  188.8 2.1 collective-permute-start.8
  193.3 2.5 collective-permute-start.10
  195.8 30.9 %shard_map.96 = (bf16[256,1792]{1,0:T(8,128)(2,1)}, bf16[256,1792]{1,0:T(8,128)(2,1)}, f32[128,4096]{1,0:T(8,128)}, f32[128,4096]{1,0:T(8,128)}, bf16[256,4096]{1,0:T(8,128)(2,1)}) custom-call(bf16[128,4096]{1,0:T(8,128)(2,1)} %copy-done.9, bf16[128,4096]{1,0:T(8,128)(2,1)} %collective-permute-done.15.refs_1_, bf16[4096,1792]{1,0:T(8,128)(2,1)} %refs_4_.4, ...), custom_call_target="tpu_custom_call" | custom-call | flops 15032385536 | bytes 67108864 | tf_op jit(solution)/shard_map/pallas_call | solution.py:178
  226.8 30.2 %collective-permute-done.10.refs_0_ = bf16[128,4096]{1,0:T(8,128)(2,1)} collective-permute-done((bf16[128,4096]{1,0:T(8,128)(2,1)}, bf16[128,4096]{1,0:T(8,128)(2,1)}, u32[]{:S(2)}, u32[]{:S(2)}) %collective-permute-start.10) | collective-permute-done | bytes 1048608 | tf_op jit(solution)/shard_map/ppermute | solution.py:250
  256.9 45.2 %collective-permute-done.13.refs_3_ = bf16[128,4096]{1,0:T(8,128)(2,1)} collective-permute-done((bf16[128,4096]{1,0:T(8,128)(2,1)}, bf16[128,4096]{1,0:T(8,128)(2,1)}, u32[]{:S(2)}, u32[]{:S(2)}) %collective-permute-start.13) | collective-permute-done | bytes 1048608 | tf_op jit(solution)/shard_map/ppermute | solution.py:250
  305.9 47.6 %shard_map.97 = (bf16[512,1792]{1,0:T(8,128)(2,1)}, bf16[512,1792]{1,0:T(8,128)(2,1)}, f32[128,4096]{1,0:T(8,128)}, f32[128,4096]{1,0:T(8,128)}, f32[128,4096]{1...) custom-call(bf16[128,4096]{1,0:T(8,128)(2,1)} %collective-permute-done.10.refs_0_, ...), custom_call_target="tpu_custom_call" | custom-call | flops 30064771072 | bytes 75497472 | tf_op jit(solution)/shard_map/pallas_call | solution.py:178
  353.5 5.4 fusion.11
  364.7 25.1 %collective-permute-done.19 = f32[128,4096]{1,0:T(8,128)} collective-permute-done((f32[128,4096]{1,0:T(8,128)}, f32[128,4096]{1,0:T(8,128)}, u32[]{:S(2)}, u32[]{:S(2)}) %collective-permute-start.19) | collective-permute-done | bytes 2097184 | tf_op jit(solution)/shard_map/ppermute | solution.py:250
  389.8 2.4 slice_add_fusion.2
  392.2 3.3 add.60
  396.0 3.5 slice_add_fusion
  399.6 3.2 add.63
  406.9 45.9 %shard_map.98 = f32[4096,1792]{1,0:T(8,128)} custom-call(bf16[256,4096]{1,0:T(8,128)(2,1)} %get-tuple-element.330.refs_0_, bf16[512,4096]{1,0:T(8,128)(2,1)} %get-tuple-element.331.refs_1_, bf16[256,4096]{1,0:T(8,128)(2,1)} %get-tuple-element.332.refs_2_, bf16[256,4096]{1,0:T(8,128)(2,1)} %copy-done.12, bf16[512,4096]{1,0:T(8,128)(2,1)} %collective-permute-done.35.refs_4_, ...), custom_call_target="tpu_custom_call" | custom-call | flops 30064771072 | bytes 53477376 | tf_op jit(solution)/shard_map/pallas_call | solution.py:218
  453.2 3.0 collective-permute-start.26
  456.3 3.2 collective-permute-start.27
  459.5 45.6 %shard_map.99 = f32[1792,4096]{1,0:T(8,128)} custom-call(bf16[256,1792]{1,0:T(8,128)(2,1)} %get-tuple-element.342.refs_0_, bf16[512,1792]{1,0:T(8,128)(2,1)} %get-tuple-element.343.refs_1_, bf16[256,1792]{1,0:T(8,128)(2,1)} %get-tuple-element.344.refs_2_, bf16[256,1792]{1,0:T(8,128)(2,1)} %copy-done.19, bf16[512,1792]{1,0:T(8,128)(2,1)} %collective-permute-done.29.refs_4_, ...), custom_call_target="tpu_custom_call" | custom-call | flops 30064771072 | bytes 53477376 | tf_op jit(solution)/shard_map/pallas_call | solution.py:218
  507.3 51.9 %collective-permute-done.25 = f32[128,4096]{1,0:T(8,128)} collective-permute-done((f32[128,4096]{1,0:T(8,128)}, f32[128,4096]{1,0:T(8,128)}, u32[]{:S(2)}, u32[]{:S(2)}) %collective-permute-start.25) | collective-permute-done | bytes 2097184 | tf_op jit(solution)/shard_map/ppermute | solution.py:250
  559.4 5.9 fusion.6
  565.4 5.1 fusion.10
  572.6 19.7 %collective-permute-done.22.u_ref = f32[96,4096]{1,0:T(8,128)} collective-permute-done((f32[96,4096]{1,0:T(8,128)S(1)}, f32[96,4096]{1,0:T(8,128)}, u32[]{:S(2)}, u32[]{:S(2)}) %collective-permute-start.22) | collective-permute-done | bytes 1572896 | tf_op jit(solution)/shard_map/ppermute | solution.py:250
  594.4 5.7 shard_map.100.refs_0_
  600.1 2.3 shard_map.101
  (126 shorter events, 32.0 us)
Async XLA Ops:
  0.7 64.4 %collective-permute-start = (bf16[4096,1792]{1,0:T(8,128)(2,1)}, bf16[4096,1792]{1,0:T(8,128)(2,1)}, u32[]{:S(2)}, u32[]{:S(2)}) collective-permute-start(bf16[4096,1792]{1,0:T(8,128)(2,1)} %refs_4_.4), channel_id=1, source_target_pairs={{0,1},{1,0},{2,3},{3,2},{4,5},{5,4},{6,7},{7,6},{8,9},{9,8},{10,11... | collective-permute-start | bytes 44040200 | tf_op jit(solution)/shard_map/ppermute | solution.py:250
  5.8 62.0 %collective-permute-start.1 = (bf16[1792,4096]{1,0:T(8,128)(2,1)}, bf16[1792,4096]{1,0:T(8,128)(2,1)}, u32[]{:S(2)}, u32[]{:S(2)}) collective-permute-start(bf16[1792,4096]{1,0:T(8,128)(2,1)} %refs_6_.1), channel_id=1, source_target_pairs={{0,1},{1,0},{2,3},{3,2},{4,5},{5,4},{6,7},{7,6},{8,9},{9,8},{10,11... | collective-permute-start | bytes 44040200 | tf_op jit(solution)/shard_map/ppermute | solution.py:250
  8.6 52.8 %collective-permute-start.3 = (bf16[128,4096]{1,0:T(8,128)(2,1)S(1)}, bf16[128,4096]{1,0:T(8,128)(2,1)}, u32[]{:S(2)}, u32[]{:S(2)}) collective-permute-start(bf16[128,4096]{1,0:T(8,128)(2,1)S(1)} %get-tuple-element.217.refs_1_), channel_id=1, source_target_pairs={{0,6},{1,7},{2,0},{3,1},{4,2},{5,3},{6,4},{7,5},{8,14},{9,15},{10,... | collective-permute-start | bytes 3145736 | tf_op jit(solution)/shard_map/ppermute | solution.py:250
  10.6 53.8 %collective-permute-start.11 = (bf16[128,4096]{1,0:T(8,128)(2,1)}, bf16[128,4096]{1,0:T(8,128)(2,1)}, u32[]{:S(2)}, u32[]{:S(2)}) collective-permute-start(bf16[128,4096]{1,0:T(8,128)(2,1)} %get-tuple-element.242), channel_id=1, source_target_pairs={{0,6},{1,7},{2,0},{3,1},{4,2},{5,3},{6,4},{7,5},{8,14},{9,15},{10,... | collective-permute-start | bytes 3145736 | tf_op jit(solution)/shard_map/ppermute | solution.py:250
  61.3 82.3 %collective-permute-start.2 = (bf16[128,4096]{1,0:T(8,128)(2,1)}, bf16[128,4096]{1,0:T(8,128)(2,1)}, u32[]{:S(2)}, u32[]{:S(2)}) collective-permute-start(bf16[128,4096]{1,0:T(8,128)(2,1)} %copy-done.4), channel_id=1, source_target_pairs={{0,6},{1,7},{2,0},{3,1},{4,2},{5,3},{6,4},{7,5},{8,14},{9,15},{10,... | collective-permute-start | bytes 3145736 | tf_op jit(solution)/shard_map/ppermute | solution.py:250
  64.5 79.2 %collective-permute-start.5 = (bf16[128,4096]{1,0:T(8,128)(2,1)}, bf16[128,4096]{1,0:T(8,128)(2,1)}, u32[]{:S(2)}, u32[]{:S(2)}) collective-permute-start(bf16[128,4096]{1,0:T(8,128)(2,1)} %copy-done.3), channel_id=1, source_target_pairs={{0,2},{1,3},{2,4},{3,5},{4,6},{5,7},{6,0},{7,1},{8,10},{9,11},{10,... | collective-permute-start | bytes 3145736 | tf_op jit(solution)/shard_map/ppermute | solution.py:250
  64.5 50.0 %collective-permute-start.6 = (bf16[128,4096]{1,0:T(8,128)(2,1)}, bf16[128,4096]{1,0:T(8,128)(2,1)}, u32[]{:S(2)}, u32[]{:S(2)}) collective-permute-start(bf16[128,4096]{1,0:T(8,128)(2,1)} %copy-done.16), channel_id=1, source_target_pairs={{0,2},{1,3},{2,4},{3,5},{4,6},{5,7},{6,0},{7,1},{8,10},{9,11},{10,... | collective-permute-start | bytes 3145736 | tf_op jit(solution)/shard_map/ppermute | solution.py:250
  65.1 49.4 %collective-permute-start.7 = (bf16[128,4096]{1,0:T(8,128)(2,1)}, bf16[128,4096]{1,0:T(8,128)(2,1)}, u32[]{:S(2)}, u32[]{:S(2)}) collective-permute-start(bf16[128,4096]{1,0:T(8,128)(2,1)} %collective-permute-done.3.refs_1_), channel_id=1, source_target_pairs={{0,6},{1,7},{2,0},{3,1},{4,2},{5,3},{6,4},{7,5},{8,14},{9,15},{10,... | collective-permute-start | bytes 3145736 | tf_op jit(solution)/shard_map/ppermute | solution.py:250
  67.8 125.5 %collective-permute-start.14 = (bf16[128,4096]{1,0:T(8,128)(2,1)}, bf16[128,4096]{1,0:T(8,128)(2,1)S(1)}, u32[]{:S(2)}, u32[]{:S(2)}) collective-permute-start(bf16[128,4096]{1,0:T(8,128)(2,1)} %collective-permute-done.12.refs_2_), channel_id=1, source_target_pairs={{0,2},{1,3},{2,4},{3,5},{4,6},{5,7},{6,0},{7,1},{8,10},{9,11},{10,... | collective-permute-start | bytes 3145736 | tf_op jit(solution)/shard_map/ppermute | solution.py:250
  114.5 81.3 %collective-permute-start.15 = (bf16[128,4096]{1,0:T(8,128)(2,1)}, bf16[128,4096]{1,0:T(8,128)(2,1)}, u32[]{:S(2)}, u32[]{:S(2)}) collective-permute-start(bf16[128,4096]{1,0:T(8,128)(2,1)} %collective-permute-done.11.refs_1_), channel_id=1, source_target_pairs={{0,6},{1,7},{2,0},{3,1},{4,2},{5,3},{6,4},{7,5},{8,14},{9,15},{10,... | collective-permute-start | bytes 3145736 | tf_op jit(solution)/shard_map/ppermute | solution.py:250
  188.8 115.3 %collective-permute-start.8 = (f32[128,4096]{1,0:T(8,128)}, f32[128,4096]{1,0:T(8,128)}, u32[]{:S(2)}, u32[]{:S(2)}) collective-permute-start(f32[128,4096]{1,0:T(8,128)} %get-tuple-element.238), channel_id=1, source_target_pairs={{0,2},{1,3},{2,4},{3,5},{4,6},{5,7},{6,0},{7,1},{8,10},{9,11},{10,... | collective-permute-start | bytes 6291464 | tf_op jit(solution)/shard_map/ppermute | solution.py:250
  190.9 114.4 %collective-permute-start.9 = (f32[128,4096]{1,0:T(8,128)}, f32[128,4096]{1,0:T(8,128)}, u32[]{:S(2)}, u32[]{:S(2)}) collective-permute-start(f32[128,4096]{1,0:T(8,128)} %get-tuple-element.240), channel_id=1, source_target_pairs={{0,6},{1,7},{2,0},{3,1},{4,2},{5,3},{6,4},{7,5},{8,14},{9,15},{10,... | collective-permute-start | bytes 6291464 | tf_op jit(solution)/shard_map/ppermute | solution.py:250
  192.1 113.2 %collective-permute-start.16 = (f32[128,4096]{1,0:T(8,128)}, f32[128,4096]{1,0:T(8,128)}, u32[]{:S(2)}, u32[]{:S(2)}) collective-permute-start(f32[128,4096]{1,0:T(8,128)} %get-tuple-element.276), channel_id=1, source_target_pairs={{0,2},{1,3},{2,4},{3,5},{4,6},{5,7},{6,0},{7,1},{8,10},{9,11},{10,... | collective-permute-start | bytes 6291464 | tf_op jit(solution)/shard_map/ppermute | solution.py:250
  193.3 63.6 %collective-permute-start.10 = (bf16[128,4096]{1,0:T(8,128)(2,1)}, bf16[128,4096]{1,0:T(8,128)(2,1)}, u32[]{:S(2)}, u32[]{:S(2)}) collective-permute-start(bf16[128,4096]{1,0:T(8,128)(2,1)} %get-tuple-element.243.refs_2_), channel_id=1, source_target_pairs={{0,6},{1,7},{2,0},{3,1},{4,2},{5,3},{6,4},{7,5},{8,14},{9,15},{10,... | collective-permute-start | bytes 3145736 | tf_op jit(solution)/shard_map/ppermute | solution.py:250
  195.8 106.3 %collective-permute-start.13 = (bf16[128,4096]{1,0:T(8,128)(2,1)}, bf16[128,4096]{1,0:T(8,128)(2,1)}, u32[]{:S(2)}, u32[]{:S(2)}) collective-permute-start(bf16[128,4096]{1,0:T(8,128)(2,1)} %get-tuple-element.244.refs_3_), channel_id=1, source_target_pairs={{0,2},{1,3},{2,4},{3,5},{4,6},{5,7},{6,0},{7,1},{8,10},{9,11},{10,... | collective-permute-start | bytes 3145736 | tf_op jit(solution)/shard_map/ppermute | solution.py:250
  302.1 56.9 %collective-permute-start.17 = (f32[128,4096]{1,0:T(8,128)}, f32[128,4096]{1,0:T(8,128)}, u32[]{:S(2)}, u32[]{:S(2)}) collective-permute-start(f32[128,4096]{1,0:T(8,128)} %get-tuple-element.278), channel_id=1, source_target_pairs={{0,6},{1,7},{2,0},{3,1},{4,2},{5,3},{6,4},{7,5},{8,14},{9,15},{10,... | collective-permute-start | bytes 6291464 | tf_op jit(solution)/shard_map/ppermute | solution.py:250
  302.1 62.2 %collective-permute-start.18 = (f32[128,4096]{1,0:T(8,128)}, f32[128,4096]{1,0:T(8,128)}, u32[]{:S(2)}, u32[]{:S(2)}) collective-permute-start(f32[128,4096]{1,0:T(8,128)} %get-tuple-element.284), channel_id=1, source_target_pairs={{0,2},{1,3},{2,4},{3,5},{4,6},{5,7},{6,0},{7,1},{8,10},{9,11},{10,... | collective-permute-start | bytes 6291464 | tf_op jit(solution)/shard_map/ppermute | solution.py:250
  304.1 85.6 %collective-permute-start.19 = (f32[128,4096]{1,0:T(8,128)}, f32[128,4096]{1,0:T(8,128)}, u32[]{:S(2)}, u32[]{:S(2)}) collective-permute-start(f32[128,4096]{1,0:T(8,128)} %get-tuple-element.286), channel_id=1, source_target_pairs={{0,6},{1,7},{2,0},{3,1},{4,2},{5,3},{6,4},{7,5},{8,14},{9,15},{10,... | collective-permute-start | bytes 6291464 | tf_op jit(solution)/shard_map/ppermute | solution.py:250
  305.3 100.1 %collective-permute-start.35 = (bf16[512,4096]{1,0:T(8,128)(2,1)}, bf16[512,4096]{1,0:T(8,128)(2,1)}, u32[]{:S(2)}, u32[]{:S(2)}) collective-permute-start(bf16[512,4096]{1,0:T(8,128)(2,1)} %get-tuple-element.331.refs_1_), channel_id=1, source_target_pairs={{0,1},{1,0},{2,3},{3,2},{4,5},{5,4},{6,7},{7,6},{8,9},{9,8},{10,11... | collective-permute-start | bytes 12582920 | tf_op jit(solution)/shard_map/ppermute | solution.py:250
  305.4 53.8 %collective-permute-start.37 = (bf16[256,1792]{1,0:T(8,128)(2,1)}, bf16[256,1792]{1,0:T(8,128)(2,1)S(1)}, u32[]{:S(2)}, u32[]{:S(2)}) collective-permute-start(bf16[256,1792]{1,0:T(8,128)(2,1)} %get-tuple-element.325), channel_id=1, source_target_pairs={{0,1},{1,0},{2,3},{3,2},{4,5},{5,4},{6,7},{7,6},{8,9},{9,8},{10,11... | collective-permute-start | bytes 2752520 | tf_op jit(solution)/shard_map/ppermute | solution.py:250
  364.1 92.2 %collective-permute-start.32 = (bf16[512,4096]{1,0:T(8,128)(2,1)}, bf16[512,4096]{1,0:T(8,128)(2,1)}, u32[]{:S(2)}, u32[]{:S(2)}) collective-permute-start(bf16[512,4096]{1,0:T(8,128)(2,1)} %get-tuple-element.349.refs_7_), channel_id=1, source_target_pairs={{0,1},{1,0},{2,3},{3,2},{4,5},{5,4},{6,7},{7,6},{8,9},{9,8},{10,11... | collective-permute-start | bytes 12582920 | tf_op jit(solution)/shard_map/ppermute | solution.py:250
  402.8 50.4 %collective-permute-start.29 = (bf16[512,1792]{1,0:T(8,128)(2,1)}, bf16[512,1792]{1,0:T(8,128)(2,1)}, u32[]{:S(2)}, u32[]{:S(2)}) collective-permute-start(bf16[512,1792]{1,0:T(8,128)(2,1)} %get-tuple-element.309), channel_id=1, source_target_pairs={{0,1},{1,0},{2,3},{3,2},{4,5},{5,4},{6,7},{7,6},{8,9},{9,8},{10,11... | collective-permute-start | bytes 5505032 | tf_op jit(solution)/shard_map/ppermute | solution.py:250
  404.2 48.7 %collective-permute-start.30 = (bf16[256,1792]{1,0:T(8,128)(2,1)}, bf16[256,1792]{1,0:T(8,128)(2,1)}, u32[]{:S(2)}, u32[]{:S(2)}) collective-permute-start(bf16[256,1792]{1,0:T(8,128)(2,1)} %get-tuple-element.311), channel_id=1, source_target_pairs={{0,1},{1,0},{2,3},{3,2},{4,5},{5,4},{6,7},{7,6},{8,9},{9,8},{10,11... | collective-permute-start | bytes 2752520 | tf_op jit(solution)/shard_map/ppermute | solution.py:250
  405.5 50.7 %collective-permute-start.31 = (bf16[256,4096]{1,0:T(8,128)(2,1)}, bf16[256,4096]{1,0:T(8,128)(2,1)}, u32[]{:S(2)}, u32[]{:S(2)}) collective-permute-start(bf16[256,4096]{1,0:T(8,128)(2,1)} %refs_6_.2), channel_id=1, source_target_pairs={{0,1},{1,0},{2,3},{3,2},{4,5},{5,4},{6,7},{7,6},{8,9},{9,8},{10,11... | collective-permute-start | bytes 6291464 | tf_op jit(solution)/shard_map/ppermute | solution.py:250
  406.5 49.7 %collective-permute-start.33 = (bf16[256,4096]{1,0:T(8,128)(2,1)}, bf16[256,4096]{1,0:T(8,128)(2,1)}, u32[]{:S(2)}, u32[]{:S(2)}) collective-permute-start(bf16[256,4096]{1,0:T(8,128)(2,1)} %get-tuple-element.350.refs_8_), channel_id=1, source_target_pairs={{0,1},{1,0},{2,3},{3,2},{4,5},{5,4},{6,7},{7,6},{8,9},{9,8},{10,11... | collective-permute-start | bytes 6291464 | tf_op jit(solution)/shard_map/ppermute | solution.py:250
  452.9 52.3 %collective-permute-start.24 = (f32[128,4096]{1,0:T(8,128)}, f32[128,4096]{1,0:T(8,128)}, u32[]{:S(2)}, u32[]{:S(2)}) collective-permute-start(f32[128,4096]{1,0:T(8,128)} %get-tuple-element.298), channel_id=1, source_target_pairs={{0,2},{1,3},{2,4},{3,5},{4,6},{5,7},{6,0},{7,1},{8,10},{9,11},{10,... | collective-permute-start | bytes 6291464 | tf_op jit(solution)/shard_map/ppermute | solution.py:250
  453.2 54.0 %collective-permute-start.26 = (f32[128,4096]{1,0:T(8,128)}, f32[128,4096]{1,0:T(8,128)}, u32[]{:S(2)}, u32[]{:S(2)}) collective-permute-start(f32[128,4096]{1,0:T(8,128)} %get-tuple-element.301), channel_id=1, source_target_pairs={{0,6},{1,7},{2,0},{3,1},{4,2},{5,3},{6,4},{7,5},{8,14},{9,15},{10,... | collective-permute-start | bytes 6291464 | tf_op jit(solution)/shard_map/ppermute | solution.py:250
  456.2 143.9 %collective-permute-start.20 = (f32[32,4096]{1,0:T(8,128)}, f32[32,4096]{1,0:T(8,128)}, u32[]{:S(2)}, u32[]{:S(2)}) collective-permute-start(f32[32,4096]{1,0:T(8,128)} %get-tuple-element.289), channel_id=1, source_target_pairs={{0,2},{1,3},{2,4},{3,5},{4,6},{5,7},{6,0},{7,1},{8,10},{9,11},{10,... | collective-permute-start | bytes 1572872 | tf_op jit(solution)/shard_map/ppermute | solution.py:250
  456.2 103.0 %collective-permute-start.25 = (f32[128,4096]{1,0:T(8,128)}, f32[128,4096]{1,0:T(8,128)}, u32[]{:S(2)}, u32[]{:S(2)}) collective-permute-start(f32[128,4096]{1,0:T(8,128)} %add.60), channel_id=1, source_target_pairs={{0,2},{1,3},{2,4},{3,5},{4,6},{5,7},{6,0},{7,1},{8,10},{9,11},{10,... | collective-permute-start | bytes 6291464 | tf_op jit(solution)/shard_map/ppermute | solution.py:250
  456.3 103.1 %collective-permute-start.27 = (f32[128,4096]{1,0:T(8,128)}, f32[128,4096]{1,0:T(8,128)}, u32[]{:S(2)}, u32[]{:S(2)}) collective-permute-start(f32[128,4096]{1,0:T(8,128)} %add.63), channel_id=1, source_target_pairs={{0,6},{1,7},{2,0},{3,1},{4,2},{5,3},{6,4},{7,5},{8,14},{9,15},{10,... | collective-permute-start | bytes 6291464 | tf_op jit(solution)/shard_map/ppermute | solution.py:250
  505.2 94.9 %collective-permute-start.21 = (f32[32,4096]{1,0:T(8,128)}, f32[32,4096]{1,0:T(8,128)}, u32[]{:S(2)}, u32[]{:S(2)}) collective-permute-start(f32[32,4096]{1,0:T(8,128)} %get-tuple-element.292), channel_id=1, source_target_pairs={{0,6},{1,7},{2,0},{3,1},{4,2},{5,3},{6,4},{7,5},{8,14},{9,15},{10,... | collective-permute-start | bytes 1572872 | tf_op jit(solution)/shard_map/ppermute | solution.py:250
  507.2 85.1 %collective-permute-start.22 = (f32[96,4096]{1,0:T(8,128)S(1)}, f32[96,4096]{1,0:T(8,128)}, u32[]{:S(2)}, u32[]{:S(2)}) collective-permute-start(f32[96,4096]{1,0:T(8,128)S(1)} %slice_add_fusion.1), channel_id=1, source_target_pairs={{0,2},{1,3},{2,4},{3,5},{4,6},{5,7},{6,0},{7,1},{8,10},{9,11},{10,... | collective-permute-start | bytes 4718600 | tf_op jit(solution)/shard_map/ppermute | solution.py:250
  (34 other events, 551.8 us)
